TPU v7x, 32 devices: a whole 2x2x4 slice. The times are simulated.
32 devices in a mesh: ctx: 8 (over z, x), head: 4 (over y, core).
Axes of the slice: x: 2, y: 2, z: 4, core: 2. Of those that a mesh axis runs over, the one named last changes fastest.
Arguments:
- queries: bfloat16 [256, 4096], P(None, 'head'), may hold values from -40 to 40
- keys: bfloat16 [16, 2048, 2048], P('ctx', None, 'head'), may hold values from -6 to 6
- values: bfloat16 [16, 2048, 2048], P('ctx', None, 'head'), may hold values from -6 to 6
- page_map: int32 [16], replicated, may hold values from 0 to 15, each once
- selected: int32 [2, 8], replicated, may hold values from 0 to 15, as said below
- residual_in: bfloat16 [256, 5376], P('head', 'ctx'), may hold values from -7 to 7
- out_weight: bfloat16 [4096, 5376], P('head', 'ctx'), may hold values from -0.09375 to 0.09375
- norm_gain: float32 [5376], P('ctx'), may hold values from 0.5 to 1.5
- gate_weight: bfloat16 [5376, 21504], P('head', 'ctx'), may hold values from -0.078125 to 0.078125
- up_weight: bfloat16 [5376, 21504], P('head', 'ctx'), may hold values from -0.078125 to 0.078125
- down_weight: bfloat16 [21504, 5376], P('ctx', 'head'), may hold values from -0.0390625 to 0.0390625
Outputs:
- layer_out: bfloat16 [256, 5376], P('ctx', 'head')
Inputs may be any that keep to these rules, and one draw needn't show every extreme that they name: `selected`: each row names 8 different logical pages, among them 16 - 1, the page that holds the block's own positions.
All inputs are finite; a program needn't handle non-finite values.
Results may differ from a plain program's by a relative error of at most 0.02.
Values may be sent and summed in bfloat16 or wider, within the bound.
A program may use at most 128 MiB of HBM per device.

v0:
```python
import jax
import jax.numpy as jnp
import functools
from jax import lax
from jax.experimental import pallas as pl
from jax.experimental.pallas import tpu as pltpu
from jax.sharding import PartitionSpec as P

D = 5376
HEAD_SIZE = 128


score_scale = 168.0 ** (-0.5)
masked_score = -1e30
norm_epsilon = 1e-06


def attention_kernel(
    logical_ref, chosen_ref, page_total, q_ref, k_ref, v_ref, mix_ref, m_ref, l_ref, acc, top, total
):
    page = pl.program_id(1)
    tile_count = chosen_ref.shape[0]
    tile_rows = q_ref.shape[0] // tile_count
    group = q_ref.shape[1] // k_ref.shape[2]
    page_len = k_ref.shape[1]
    offset = page_len - q_ref.shape[0]
    f32 = jnp.float32

    @pl.when(page == 0)
    def _():
        acc[...] = jnp.zeros_like(acc)
        top[...] = jnp.full_like(top, masked_score)
        total[...] = jnp.zeros_like(total)

    causal = logical_ref[page] == page_total - 1

    def visit(t, masked):
        rows = slice(t * tile_rows, (t + 1) * tile_rows)
        for g in range(group):
            cols = slice(g * HEAD_SIZE, (g + 1) * HEAD_SIZE)
            scores = (
                lax.dot_general(
                    q_ref[rows, cols],
                    k_ref[0],
                    (((1,), (1,)), ((), ())),
                    preferred_element_type=f32,
                )
                * score_scale
            )
            if masked:
                position = offset + t * tile_rows + lax.broadcasted_iota(jnp.int32, scores.shape, 0)
                key = lax.broadcasted_iota(jnp.int32, scores.shape, 1)
                scores = jnp.where(key <= position, scores, masked_score)
            old = top[g, rows, :1]
            new = jnp.maximum(old, jnp.max(scores, axis=1, keepdims=True))
            weights = jnp.exp(scores - new)
            keep = jnp.exp(old - new)
            total[g, rows] = total[g, rows] * keep + jnp.sum(weights, axis=1, keepdims=True)
            top[g, rows] = jnp.broadcast_to(new, (tile_rows, 128))
            acc[rows, cols] = acc[rows, cols] * keep + jnp.dot(
                weights.astype(jnp.bfloat16), v_ref[0], preferred_element_type=f32
            )

    for t in range(tile_count):
        picked = chosen_ref[t, page] != 0
        pl.when(jnp.logical_and(picked, causal))(functools.partial(visit, t, True))
        pl.when(jnp.logical_and(picked, jnp.logical_not(causal)))(
            functools.partial(visit, t, False)
        )

    @pl.when(page == pl.num_programs(1) - 1)
    def _():
        mix_ref[...] = acc[...].astype(jnp.bfloat16)
        lane = lax.broadcasted_iota(jnp.int32, m_ref.shape[1:], 1)
        maxima = jnp.zeros(m_ref.shape[1:], f32)
        sums = jnp.zeros(m_ref.shape[1:], f32)
        for g in range(group):
            maxima = jnp.where(lane == g, top[g], maxima)
            sums = jnp.where(lane == g, total[g], sums)
        m_ref[0] = maxima
        l_ref[0] = sums


def owner_pass(queries, keys, values, page_map, selected, ctx_index, ctx_count):
    pages_local, page_len, kv_width = keys.shape
    row_count, query_width = queries.shape
    kv_local = kv_width // HEAD_SIZE
    group = query_width // kv_width
    tile_count = selected.shape[0]
    page_total = pages_local * ctx_count
    slot_ids = ctx_index * pages_local + jnp.arange(pages_local, dtype=jnp.int32)
    all_pages = jnp.arange(page_total, dtype=jnp.int32)
    logical = jnp.sum(
        jnp.where(page_map[None, :] == slot_ids[:, None], all_pages[None, :], 0), axis=1
    )
    chosen = jnp.any(selected[:, None, :] == logical[None, :, None], axis=2).astype(jnp.int32)
    stat = jax.ShapeDtypeStruct((kv_local, row_count, 128), jnp.float32)
    stat_spec = pl.BlockSpec((1, row_count, 128), lambda k, p, a, b: (k, 0, 0))
    kv_spec = pl.BlockSpec((1, page_len, HEAD_SIZE), lambda k, p, a, b: (p, 0, k))
    q_spec = pl.BlockSpec((row_count, group * HEAD_SIZE), lambda k, p, a, b: (0, k))

    def kernel(logical_ref, chosen_ref, *refs):
        attention_kernel(logical_ref, chosen_ref, page_total, *refs)

    mixture, top, total = pl.pallas_call(
        kernel,
        grid_spec=pltpu.PrefetchScalarGridSpec(
            num_scalar_prefetch=2,
            grid=(kv_local, pages_local),
            in_specs=[q_spec, kv_spec, kv_spec],
            out_specs=(q_spec, stat_spec, stat_spec),
            scratch_shapes=[
                pltpu.VMEM((row_count, group * HEAD_SIZE), jnp.float32),
                pltpu.VMEM((group, row_count, 128), jnp.float32),
                pltpu.VMEM((group, row_count, 128), jnp.float32),
            ],
        ),
        out_shape=(jax.ShapeDtypeStruct((row_count, query_width), jnp.bfloat16), stat, stat),
    )(logical.astype(jnp.int32), chosen, queries, keys, values)

    def heads(stacked):
        return stacked[:, :, :group].transpose(1, 0, 2).reshape(row_count, kv_local * group)

    return heads(top), heads(total), mixture


MESH = pl.DeviceIdType.MESH
CORES = 2


def column_tile(width):
    for tile in (896, 768, 640, 512, 384, 256, 128):
        if width % tile == 0:
            return tile
    return width


def flat(block, rows):
    if block.shape[1] % 16:
        return block.astype(jnp.float32).reshape(rows, -1).astype(jnp.bfloat16)
    return block.reshape(rows, -1)


def tail_kernel(
    C,
    H,
    mix_ref,
    stat_ref,
    res_ref,
    gain_ref,
    ow_hbm,
    gw_hbm,
    uw_hbm,
    dw_hbm,
    mlp_ref,
    own_ref,
    ow,
    gw,
    uw,
    dw,
    mix_in,
    stat_in,
    att,
    po,
    po_in,
    u_out,
    st_out,
    ss,
    ublk,
    own_st,
    first,
    first_in,
    second,
    second_in,
    hid,
    acc,
    part,
    part_in,
    w_sem,
    mix_s,
    mix_r,
    stat_s,
    stat_r,
    att_s,
    att_r,
    po_s,
    po_r,
    u_s,
    u_r,
    st_s,
    st_r,
    ss_s,
    ss_r,
    f_s,
    f_r,
    g_s,
    g_r,
    h_s,
    h_r,
    fw_s,
    part_s,
    part_r,
):
    c = lax.axis_index("ctx")
    h = lax.axis_index("head")
    Y = H // CORES
    y = h // CORES
    core = h % CORES
    partner = y * CORES + (CORES - 1 - core)
    R = mix_ref.shape[1]
    rows = C * R
    rb = C // H
    bph = C // H
    width = ow.shape[1]
    head_rows = rows // H
    heads = mix_ref.shape[2] // HEAD_SIZE
    tiles, _, _, _, _, tile = first.shape
    f32 = jnp.float32
    bf16 = jnp.bfloat16

    def remote(src, dst, send_sem, recv_sem, ctx, head):
        return pltpu.make_async_remote_copy(
            src_ref=src,
            dst_ref=dst,
            send_sem=send_sem,
            recv_sem=recv_sem,
            device_id=(ctx, head),
            device_id_type=MESH,
        )

    sent = []

    def send(*args):
        copy = remote(*args)
        copy.start()
        sent.append(copy)

    loads = [
        pltpu.make_async_copy(src, dst, w_sem.at[i])
        for i, (src, dst) in enumerate(
            ((ow_hbm, ow), (gw_hbm, gw), (uw_hbm, uw), (dw_hbm, dw))
        )
    ]
    for load in loads:
        load.start()

    for d in range(1, C):
        peer = (c + d) % C
        send(stat_ref.at[peer], stat_in.at[c], stat_s.at[d], stat_r.at[c], peer, h)
        send(mix_ref.at[peer], mix_in.at[c], mix_s.at[d], mix_r.at[c], peer, h)
    stat_in[c] = stat_ref[c]
    mix_in[c] = mix_ref[c]
    for d in range(1, C):
        peer = (c + C - d) % C
        remote(stat_in.at[peer], stat_in.at[peer], stat_s.at[d], stat_r.at[peer], peer, h).wait_recv()
        remote(mix_in.at[peer], mix_in.at[peer], mix_s.at[d], mix_r.at[peer], peer, h).wait_recv()
    maxima = [stat_in[k][:, :heads] for k in range(C)]
    top = functools.reduce(jnp.maximum, maxima)
    scales = [jnp.exp(m - top) for m in maxima]
    total = sum(stat_in[k][:, heads : 2 * heads] * scales[k] for k in range(C))
    inverse = 1.0 / total
    for g in range(heads):
        cols = slice(g * HEAD_SIZE, (g + 1) * HEAD_SIZE)
        mixed = sum(mix_in[k, :, cols].astype(f32) * scales[k][:, g : g + 1] for k in range(C))
        att[c, :, cols] = (mixed * inverse[:, g : g + 1]).astype(bf16)

    for d in range(1, C):
        peer = (c + d) % C
        send(att.at[c], att.at[c], att_s.at[d], att_r.at[c], peer, h)
    loads[0].wait()
    for d in range(1, C):
        peer = (c + C - d) % C
        remote(att.at[peer], att.at[peer], att_s.at[d], att_r.at[peer], peer, h).wait_recv()
    projected = jnp.dot(flat(att[...], rows), ow[...], preferred_element_type=f32)
    po[...] = projected.reshape(H, head_rows, width).astype(bf16)

    for d in range(1, H):
        peer = (h + d) % H
        send(po.at[peer], po_in.at[h], po_s.at[d], po_r.at[h], c, peer)
    po_in[h] = po[h]
    for d in range(1, H):
        peer = (h + H - d) % H
        remote(po_in.at[peer], po_in.at[peer], po_s.at[d], po_r.at[peer], c, peer).wait_recv()
    projected = sum(po_in[k].astype(f32) for k in range(H))
    stream = (res_ref[...].astype(f32) + projected).astype(bf16).astype(f32)
    st_out[...] = stream.reshape(rb, R, width).astype(bf16)
    u_out[...] = (stream * gain_ref[...]).reshape(rb, R, width).astype(bf16)
    squares = jnp.sum(stream * stream, axis=1, keepdims=True)
    ss[c] = jnp.broadcast_to(squares, (head_rows, 128))

    block_head = c // bph
    block_part = c % bph
    u_dst = ublk.at[block_part, pl.ds(h * rb, rb)]
    kept = []
    for d in range(C):
        peer = (c + d) % C
        copy = remote(u_out, u_dst, u_s.at[d], u_r.at[block_part, h], peer, block_head)
        if d == 0:
            kept.append((block_head != h, copy))
            pl.when(block_head != h)(copy.start)

            @pl.when(block_head == h)
            def _():
                ublk[block_part, pl.ds(h * rb, rb)] = u_out[...]

        else:
            copy.start()
            sent.append(copy)
    for d in range(1, C):
        peer = (c + d) % C
        send(ss.at[c], ss.at[c], ss_s.at[d], ss_r.at[c], peer, h)
    for i in range(rb):
        owner = h * rb + i
        other = jnp.logical_or(owner != c, block_head != h)
        copy = remote(
            st_out.at[i], own_st.at[block_part], st_s.at[i], st_r.at[block_part], owner, block_head
        )
        kept.append((other, copy))
        pl.when(other)(copy.start)

        @pl.when(jnp.logical_not(other))
        def _(i=i):
            own_st[block_part] = st_out[i]

    for j in range(bph):
        for k in range(H):
            source = h * bph + j
            block = ublk.at[j, pl.ds(k * rb, rb)]
            arrival = remote(block, block, u_s.at[0], u_r.at[j, k], source, k)
            pl.when(jnp.logical_or(source != c, h != k))(arrival.wait_recv)
    loads[1].wait()
    loads[2].wait()

    def matmul(i, which, weight):
        cols = slice(i * tile, (i + 1) * tile)
        value = None
        for j in range(bph):
            term = jnp.dot(
                flat(ublk[j], rows),
                weight[j * width : (j + 1) * width, cols],
                preferred_element_type=f32,
            )
            value = term if value is None else value + term
        first[i, which] = value.reshape(Y, CORES, head_rows, tile).swapaxes(0, 1).astype(bf16)
        send(
            first.at[i, which, CORES - 1 - core],
            first_in.at[i, which],
            f_s.at[i, which],
            f_r.at[i, which],
            c,
            partner,
        )

    def middle(i, which):
        remote(
            first_in.at[i, which], first_in.at[i, which], f_s.at[i, which], f_r.at[i, which], c, partner
        ).wait_recv()
        both = first[i, which, core].astype(f32) + first_in[i, which].astype(f32)
        second[i, which] = both.astype(bf16)
        for d in range(1, Y):
            peer = (y + d) % Y
            send(
                second.at[i, which, peer],
                second_in.at[i, which, y],
                g_s.at[i, which, d],
                g_r.at[i, which, y],
                c,
                peer * CORES + core,
            )

    def finish(i, inverse_rms):
        sums = []
        for which in range(2):
            value = second[i, which, y].astype(f32)
            for d in range(1, Y):
                peer = (y + Y - d) % Y
                slot = second_in.at[i, which, peer]
                remote(
                    slot, slot, g_s.at[i, which, d], g_r.at[i, which, peer], c, peer * CORES + core
                ).wait_recv()
                value = value + second_in[i, which, peer].astype(f32)
            sums.append(value * inverse_rms)
        hid[i, h] = (jax.nn.gelu(sums[0], approximate=True) * sums[1]).astype(bf16)
        send(hid.at[i, h], hid.at[i, h], h_s.at[i, 0], h_r.at[i, h], c, partner)
        for d in range(1, Y):
            peer = ((y + d) % Y) * CORES + core
            send(hid.at[i, h], hid.at[i, h], h_s.at[i, d], h_r.at[i, h], c, peer)

    def forward(i):
        for d in range(1, Y):
            origin = ((y + Y - d) % Y) * CORES + core
            slot = hid.at[i, origin]
            remote(slot, slot, h_s.at[i, d], h_r.at[i, origin], c, origin).wait_recv()
            send(slot, slot, fw_s.at[i, d], h_r.at[i, origin], c, partner)

    def down(i):
        for d in range(Y):
            origin = ((y + Y - d) % Y) * CORES + (CORES - 1 - core)
            slot = hid.at[i, origin]
            remote(slot, slot, h_s.at[i, 0], h_r.at[i, origin], c, partner).wait_recv()
        term = jnp.dot(
            flat(hid[i], rows), dw[i * tile : (i + 1) * tile, :], preferred_element_type=f32
        )
        if i == 0:
            acc[...] = term
        else:
            acc[...] += term

    steps = [(i, which) for i in range(tiles) for which in range(2)]
    for n, (i, which) in enumerate(steps):
        matmul(i, which, (gw, uw)[which])
        if n:
            middle(*steps[n - 1])
    middle(*steps[-1])
    for d in range(1, C):
        peer = (c + C - d) % C
        remote(ss.at[peer], ss.at[peer], ss_s.at[d], ss_r.at[peer], peer, h).wait_recv()
    squares = sum(ss[k] for k in range(C))
    inverse_rms = lax.rsqrt(squares[:, :1] / (C * width) + norm_epsilon)
    loads[3].wait()
    for i in range(tiles):
        finish(i, inverse_rms)
        if i:
            forward(i - 1)
    forward(tiles - 1)
    for i in range(tiles):
        down(i)
    part[...] = acc[...].reshape(C, R, acc.shape[1]).astype(bf16)

    for d in range(1, C):
        peer = (c + d) % C
        send(part.at[peer], part_in.at[c], part_s.at[d], part_r.at[c], peer, h)
    part_in[c] = part[c]
    for j in range(bph):
        source = h * bph + j
        arrival = remote(own_st.at[j], own_st.at[j], st_s.at[0], st_r.at[j], source, c // rb)
        pl.when(jnp.logical_or(source != c, c // rb != h))(arrival.wait_recv)
    own_ref[...] = own_st[...]
    for d in range(1, C):
        peer = (c + C - d) % C
        remote(part_in.at[peer], part_in.at[peer], part_s.at[d], part_r.at[peer], peer, h).wait_recv()
    mlp_ref[...] = sum(part_in[k].astype(f32) for k in range(C))
    for copy in sent:
        copy.wait_send()
    for condition, copy in kept:
        pl.when(condition)(copy.wait_send)


def tail(C, H, mixture, stats, residual_in, norm_gain, out_weight, gate_weight, up_weight, down_weight):
    rows, query_width = mixture.shape
    R = rows // C
    width = out_weight.shape[1]
    hidden = gate_weight.shape[1]
    out_width = down_weight.shape[1]
    rb = C // H
    bph = C // H
    Y = H // CORES
    head_rows = rows // H
    tile = column_tile(hidden)
    tiles = hidden // tile
    bf16 = jnp.bfloat16
    vmem = pl.BlockSpec(memory_space=pltpu.VMEM)
    hbm = pl.BlockSpec(memory_space=pl.ANY)
    V = pltpu.VMEM
    S = pltpu.SemaphoreType.DMA
    return pl.pallas_call(
        functools.partial(tail_kernel, C, H),
        out_shape=(
            jax.ShapeDtypeStruct((R, out_width), jnp.float32),
            jax.ShapeDtypeStruct((bph, R, width), bf16),
        ),
        in_specs=[vmem] * 4 + [hbm] * 4,
        out_specs=(vmem, vmem),
        scratch_shapes=[
            V(out_weight.shape, bf16),
            V(gate_weight.shape, bf16),
            V(up_weight.shape, bf16),
            V(down_weight.shape, bf16),
            V((C, R, query_width), bf16),
            V((C, R, 128), jnp.float32),
            V((C, R, query_width), bf16),
            V((H, head_rows, width), bf16),
            V((H, head_rows, width), bf16),
            V((rb, R, width), bf16),
            V((rb, R, width), bf16),
            V((C, head_rows, 128), jnp.float32),
            V((bph, C, R, width), bf16),
            V((bph, R, width), bf16),
            V((tiles, 2, CORES, Y, head_rows, tile), bf16),
            V((tiles, 2, Y, head_rows, tile), bf16),
            V((tiles, 2, Y, head_rows, tile), bf16),
            V((tiles, 2, Y, head_rows, tile), bf16),
            V((tiles, H, head_rows, tile), bf16),
            V((rows, out_width), jnp.float32),
            V((C, R, out_width), bf16),
            V((C, R, out_width), bf16),
            S((4,)),
            S((C,)),
            S((C,)),
            S((C,)),
            S((C,)),
            S((C,)),
            S((C,)),
            S((H,)),
            S((H,)),
            S((C,)),
            S((bph, H)),
            S((rb,)),
            S((bph,)),
            S((C,)),
            S((C,)),
            S((tiles, 2)),
            S((tiles, 2)),
            S((tiles, 2, Y)),
            S((tiles, 2, Y)),
            S((tiles, Y)),
            S((tiles, H)),
            S((tiles, Y)),
            S((C,)),
            S((C,)),
        ],
        compiler_params=pltpu.CompilerParams(
            has_side_effects=True, vmem_limit_bytes=60 * 2**20
        ),
    )(
        mixture.reshape(C, R, query_width),
        stats.reshape(C, R, 128),
        residual_in,
        norm_gain.reshape(1, width),
        out_weight,
        gate_weight,
        up_weight,
        down_weight,
    )


def shards(
    queries,
    keys,
    values,
    page_map,
    selected,
    residual_in,
    out_weight,
    norm_gain,
    gate_weight,
    up_weight,
    down_weight,
):
    ctx_index = lax.axis_index("ctx")
    C = lax.axis_size("ctx")
    H = lax.axis_size("head")
    row_max, row_total, mixture = owner_pass(
        queries, keys, values, page_map, selected, ctx_index, C
    )
    stats = jnp.concatenate([row_max, row_total], axis=1)
    stats = jnp.pad(stats, ((0, 0), (0, 128 - stats.shape[1])))
    mlp_out, own_stream = tail(
        C,
        H,
        mixture.astype(jnp.bfloat16),
        stats,
        residual_in,
        norm_gain,
        out_weight,
        gate_weight,
        up_weight,
        down_weight,
    )
    own_stream = jnp.concatenate([own_stream[j] for j in range(own_stream.shape[0])], axis=1)
    return (own_stream.astype(jnp.float32) + mlp_out).astype(jnp.bfloat16)


def solution(mesh):
    in_specs = (
        P(None, "head"),
        P("ctx", None, "head"),
        P("ctx", None, "head"),
        P(),
        P(),
        P("head", "ctx"),
        P("head", "ctx"),
        P("ctx"),
        P("head", "ctx"),
        P("head", "ctx"),
        P("ctx", "head"),
    )
    out_specs = P("ctx", "head")
    return jax.shard_map(shards, mesh=mesh, in_specs=in_specs, out_specs=out_specs, check_vma=False)
```

profile of v0, /device:TPU:18, one launch (start us, length us, event | category | flops | bytes accessed | tf_op | source)
XLA Modules:
  0.0 157.5 jit_solution(7446088268381944094)
XLA Ops:
  0.0 0.0 copy-start
  0.0 0.9 fusion.logical_ref
  0.9 0.0 copy-start.1
  1.0 0.9 compare_reduce_fusion
  1.8 0.6 convert_element_type.11.chosen_ref
  2.4 1.3 reshape.26.gain_ref
  3.7 0.0 copy-done.1
  3.7 7.8 %shard_map.109 = (bf16[256,1024]{1,0:T(8,128)(2,1)}, f32[4,256,128]{2,1,0:T(8,128)}, f32[4,256,128]{2,1,0:T(8,128)}) custom-call(s32[2]{0:T(128)} %copy-done.1, s32[2,2]{1,0:T(2,128)} %convert_element_type.11.chosen_ref, bf16[256,1024]{1,0:T(8,128)(2,1)} %refs_0_.1, bf16[2,2048,512]{2,1,0:T(8,128)(2,1)} %refs_1_.1, bf16[2,2048,512]{2,1,0:T(8,128)(2,1)} %refs_2_.1), custom_call_target="tpu_custom_call" | custom-call | tf_op jit(solution)/shard_map/pallas_call | solution.py:105
  11.5 1.3 slice_bitcast_fusion
  12.8 0.2 copy.20
  13.0 0.2 copy.19
  13.2 0.1 copy.24
  13.3 0.7 pad.4.clone
  14.0 0.0 copy-done
  14.0 1.6 %copy.22.ow_hbm = bf16[1024,672]{1,0:T(8,128)(2,1)} copy(bf16[1024,672]{0,1:T(8,128)(2,1)S(1)} %copy-done) | data formatting | bytes 2752512 | tf_op args[6]
  15.6 10.8 %copy.23.dw_hbm = bf16[2688,1344]{1,0:T(8,128)(2,1)} copy(bf16[2688,1344]{0,1:T(8,128)(2,1)} %param.21) | data formatting | bytes 14450688 | tf_op args[10]
  26.4 128.7 %shard_map.110 = (f32[32,1344]{1,0:T(8,128)}, bf16[2,32,672]{2,1,0:T(8,128)(2,1)}) custom-call(bf16[8,32,1024]{2,1,0:T(8,128)(2,1)} %bitcast.15, f32[8,32,128]{2,1,0:T(8,128)} %bitcast.14, bf16[64,672]{1,0:T(8,128)(2,1)} %res_ref.1, f32[1,672]{1,0:T(1,128)} %reshape.26.gain_ref, bf16[1024,672]{1,0:T(8,128)(2,1)} %copy.22.ow_hbm, bf16[1344,2688]{1,0:T(8,128)(2,1)} %gw_hbm.1, ...), custom_call_target="tpu_custom_call" | custom-call | tf_op jit(solution)/shard_map/pallas_call | solution.py:466
  155.1 0.8 slice_bitcast_fusion.3
  155.9 1.6 %add_convert_fusion = bf16[32,1344]{1,0:T(8,128)(2,1)} fusion(f32[32,1344]{1,0:T(8,128)} %get-tuple-element.14, bf16[32,672]{1,0:T(8,128)(2,1)S(1)} %get-tuple-element.16, bf16[32,672]{1,0:T(8,128)(2,1)S(1)} %get-tuple-element.15), kind=kLoop, calls=%fused_computation.2 | loop fusion | flops 258048 | bytes 344064 | tf_op jit(solution)/shard_map/convert_element_type | solution.py:571
  (4 shorter events, 0.0 us)
Async XLA Ops:
  0.0 14.0 %copy-start = (bf16[1024,672]{0,1:T(8,128)(2,1)S(1)}, bf16[1024,672]{0,1:T(8,128)(2,1)}, u32[]{:S(2)}) copy-start(bf16[1024,672]{0,1:T(8,128)(2,1)} %param.17) | copy-start | bytes 4128772
  0.9 2.7 %copy-start.1 = (s32[2]{0:T(128)}, s32[2]{0:T(128)S(1)}, u32[]{:S(2)}) copy-start(s32[2]{0:T(128)S(1)} %fusion.logical_ref) | copy-start | bytes 28
where the time goes:
time: 158 us
  Pallas kernels  136 us (86%)
  local copies, waits for them, and re-layouts  16.9 us (11%)
  other arithmetic  4.06 us (3%)
    pallas_call x1, Pallas kernels, tail(): pl.pallas_call(functools.partial(tail_kernel, C, H), out_shape=(jax.Shape...  129 us
    unnamed x7, local copies, waits for them, and re-layouts  12.5 us
    pallas_call x1, Pallas kernels, owner_pass(): pl.pallas_call(kernel, grid_spec=pltpu.PrefetchScalarGridSpec(num_scalar_...  7.8 us

commit v1 on v0

--- a/solution.py
+++ b/solution.py
@@ -211,7 +211,7 @@
     rows = C * R
     rb = C // H
     bph = C // H
-    width = ow.shape[1]
+    width = ow.shape[0]
     head_rows = rows // H
     heads = mix_ref.shape[2] // HEAD_SIZE
     tiles, _, _, _, _, tile = first.shape
@@ -271,7 +271,9 @@
     for d in range(1, C):
         peer = (c + C - d) % C
         remote(att.at[peer], att.at[peer], att_s.at[d], att_r.at[peer], peer, h).wait_recv()
-    projected = jnp.dot(flat(att[...], rows), ow[...], preferred_element_type=f32)
+    projected = lax.dot_general(
+        flat(att[...], rows), ow[...], (((1,), (1,)), ((), ())), preferred_element_type=f32
+    )
     po[...] = projected.reshape(H, head_rows, width).astype(bf16)
 
     for d in range(1, H):
@@ -398,8 +400,11 @@
             origin = ((y + Y - d) % Y) * CORES + (CORES - 1 - core)
             slot = hid.at[i, origin]
             remote(slot, slot, h_s.at[i, 0], h_r.at[i, origin], c, partner).wait_recv()
-        term = jnp.dot(
-            flat(hid[i], rows), dw[i * tile : (i + 1) * tile, :], preferred_element_type=f32
+        term = lax.dot_general(
+            flat(hid[i], rows),
+            dw[:, i * tile : (i + 1) * tile],
+            (((1,), (1,)), ((), ())),
+            preferred_element_type=f32,
         )
         if i == 0:
             acc[...] = term
@@ -452,6 +457,8 @@
     width = out_weight.shape[1]
     hidden = gate_weight.shape[1]
     out_width = down_weight.shape[1]
+    out_weight = out_weight.T
+    down_weight = down_weight.T
     rb = C // H
     bph = C // H
     Y = H // CORES

time: 158 us -> 144 us (0.911)
  the two profiles are of different devices: /device:TPU:18 before, /device:TPU:22 now
where the time goes in v1:
time: 144 us; the launch traced here: 141 us
  Pallas kernels  133 us (92%)
  other arithmetic  3.93 us (3%)
  local copies, waits for them, and re-layouts  3.85 us (3%)
    pallas_call x1, Pallas kernels, tail(): pl.pallas_call(functools.partial(tail_kernel, C, H), out_shape=(jax.Shape...  114 us
    pallas_call x1, Pallas kernels, owner_pass(): pl.pallas_call(kernel, grid_spec=pltpu.PrefetchScalarGridSpec(num_scalar_...  19.1 us

profile of v1, /device:TPU:22, one launch (start us, length us, event | category | flops | bytes accessed | tf_op | source)
XLA Modules:
  0.0 140.7 jit_solution(9379236907914226200)
XLA Ops:
  0.0 0.0 copy-start
  0.0 0.8 fusion.logical_ref
  0.9 0.0 copy-start.1
  0.9 0.9 compare_reduce_fusion
  1.7 0.6 convert_element_type.11.chosen_ref
  2.3 0.0 copy-done.1
  2.3 19.1 %shard_map.109 = (bf16[256,1024]{1,0:T(8,128)(2,1)}, f32[4,256,128]{2,1,0:T(8,128)}, f32[4,256,128]{2,1,0:T(8,128)}) custom-call(s32[2]{0:T(128)} %copy-done.1, s32[2,2]{1,0:T(2,128)} %convert_element_type.11.chosen_ref, bf16[256,1024]{1,0:T(8,128)(2,1)} %refs_0_.1, bf16[2,2048,512]{2,1,0:T(8,128)(2,1)} %refs_1_.1, bf16[2,2048,512]{2,1,0:T(8,128)(2,1)} %refs_2_.1), custom_call_target="tpu_custom_call" | custom-call | tf_op jit(solution)/shard_map/pallas_call | solution.py:105
  21.4 1.3 slice_bitcast_fusion
  22.6 0.2 copy.16
  22.8 0.2 copy.15
  23.1 0.1 copy.18
  23.2 0.7 pad.4.clone
  23.8 0.0 copy-done
  23.8 0.6 reshape.26.gain_ref
  24.4 113.8 %shard_map.110 = (f32[32,1344]{1,0:T(8,128)}, bf16[2,32,672]{2,1,0:T(8,128)(2,1)}) custom-call(bf16[8,32,1024]{2,1,0:T(8,128)(2,1)} %bitcast.19, f32[8,32,128]{2,1,0:T(8,128)} %bitcast.18, bf16[64,672]{1,0:T(8,128)(2,1)} %res_ref.1, f32[1,672]{1,0:T(1,128)} %reshape.26.gain_ref, bf16[672,1024]{1,0:T(8,128)(2,1)} %bitcast.17, bf16[1344,2688]{1,0:T(8,128)(2,1)} %gw_hbm.1, ...), custom_call_target="tpu_custom_call" | custom-call | tf_op jit(solution)/shard_map/pallas_call | solution.py:473
  138.3 0.8 slice_bitcast_fusion.3
  139.1 1.6 %add_convert_fusion = bf16[32,1344]{1,0:T(8,128)(2,1)} fusion(f32[32,1344]{1,0:T(8,128)} %get-tuple-element.14, bf16[32,672]{1,0:T(8,128)(2,1)S(1)} %get-tuple-element.16, bf16[32,672]{1,0:T(8,128)(2,1)S(1)} %get-tuple-element.15), kind=kLoop, calls=%fused_computation.2 | loop fusion | flops 258048 | bytes 344064 | tf_op jit(solution)/shard_map/convert_element_type | solution.py:578
  (4 shorter events, 0.0 us)
Async XLA Ops:
  0.0 23.8 %copy-start = (f32[672]{0:T(1024)S(1)}, f32[672]{0:T(1024)}, u32[]{:S(2)}) copy-start(f32[672]{0:T(1024)} %param.18) | copy-start | bytes 8068
  0.9 1.4 %copy-start.1 = (s32[2]{0:T(128)}, s32[2]{0:T(128)S(1)}, u32[]{:S(2)}) copy-start(s32[2]{0:T(128)S(1)} %fusion.logical_ref) | copy-start | bytes 28

commit v2 on v1

--- a/solution.py
+++ b/solution.py
@@ -541,6 +541,707 @@
     )
 
 
+LOG2E = 1.4426950408889634
+
+
+def fused_kernel(
+    C,
+    H,
+    NP,
+    map_ref,
+    sel_ref,
+    q_ref,
+    res_ref,
+    gain_ref,
+    k_hbm,
+    v_hbm,
+    ow_hbm,
+    gw_hbm,
+    uw_hbm,
+    dw_hbm,
+    out_ref,
+    k_buf,
+    v_buf,
+    ow,
+    gw,
+    uw,
+    dw,
+    mix_out,
+    mix_in,
+    lse_out,
+    lse_in,
+    att,
+    po_out,
+    po_in,
+    res_in,
+    st,
+    u,
+    ss_out,
+    ss_in,
+    ss_mid,
+    ss_last,
+    first,
+    first_in,
+    second,
+    second_in,
+    hid,
+    acc,
+    part,
+    part_in,
+    kv_sem,
+    w_sem,
+    mix_s,
+    mix_r,
+    lse_s,
+    lse_r,
+    att_s,
+    att_r,
+    po_s,
+    po_r,
+    res_s,
+    res_r,
+    u_s,
+    u_r,
+    ss_s,
+    ss_r,
+    f_s,
+    f_r,
+    g_s,
+    g_r,
+    h_s,
+    h_r,
+    fw_s,
+    part_s,
+    part_r,
+):
+    c = lax.axis_index("ctx")
+    h = lax.axis_index("head")
+    X = C // H
+    Z = C // X
+    z = c // X
+    x = c % X
+    Y = H // CORES
+    y = h // CORES
+    core = h % CORES
+    partner = y * CORES + (CORES - 1 - core)
+    _, NQ, RC, query_width = q_ref.shape
+    rows = C * RC
+    hr = rows // H
+    kv, pages, page_len, _ = k_buf.shape
+    group = query_width // (kv * HEAD_SIZE)
+    gw_cols = group * HEAD_SIZE
+    tile_count = sel_ref.shape[0]
+    tile_rows = NQ * rows // tile_count
+    offset = page_len - NQ * rows
+    page_total = map_ref.shape[0]
+    width = ow.shape[0]
+    tile = first.shape[-1]
+    tiles = first.shape[1]
+    RP = rows // NP
+    f32 = jnp.float32
+    bf16 = jnp.bfloat16
+    owner = h == z
+    visitor = h != z
+
+    def remote(src, dst, send_sem, recv_sem, ctx, head):
+        return pltpu.make_async_remote_copy(
+            src_ref=src,
+            dst_ref=dst,
+            send_sem=send_sem,
+            recv_sem=recv_sem,
+            device_id=(ctx, head),
+            device_id_type=MESH,
+        )
+
+    sent = []
+    kept = []
+
+    def send(*args):
+        copy = remote(*args)
+        copy.start()
+        sent.append(copy)
+
+    def send_if(condition, *args):
+        copy = remote(*args)
+        pl.when(condition)(copy.start)
+        kept.append((condition, copy))
+
+    def kv_load(j):
+        lanes = pl.ds(pl.multiple_of(j * HEAD_SIZE, HEAD_SIZE), HEAD_SIZE)
+        return (
+            pltpu.make_async_copy(k_hbm.at[:, :, lanes], k_buf.at[j], kv_sem.at[0, j]),
+            pltpu.make_async_copy(v_hbm.at[:, :, lanes], v_buf.at[j], kv_sem.at[1, j]),
+        )
+
+    for j in range(kv):
+        for load in kv_load(j):
+            load.start()
+    loads = [
+        pltpu.make_async_copy(src, dst, w_sem.at[i])
+        for i, (src, dst) in enumerate(
+            ((ow_hbm, ow), (gw_hbm, gw), (uw_hbm, uw), (dw_hbm, dw))
+        )
+    ]
+    for load in loads:
+        load.start()
+
+    send_if(visitor, res_ref, res_in.at[h], res_s.at[0], res_r.at[h], c, z)
+    res_in[h] = res_ref[...]
+
+    facts = []
+    for p in range(pages):
+        slot = c * pages + p
+        logical = jnp.int32(0)
+        for j in range(page_total):
+            logical = logical + jnp.where(map_ref[j] == slot, j, 0)
+        picks = []
+        for t in range(tile_count):
+            hits = jnp.int32(0)
+            for i in range(sel_ref.shape[1]):
+                hits = hits + jnp.where(sel_ref[t, i] == logical, 1, 0)
+            picks.append(jnp.where(hits > 0, 0.0, masked_score).astype(f32))
+        reach = jnp.where(logical == page_total - 1, 0, page_len)
+        facts.append((reach, picks))
+
+    index = lax.broadcasted_iota(jnp.int32, (group * rows, 1), 0) & (rows - 1)
+    shift = RC.bit_length() - 1
+    base_row = (index >> shift) * (NQ * RC) + (index & (RC - 1))
+    eye = lax.broadcasted_iota(jnp.int32, (rows, rows), 0) == lax.broadcasted_iota(
+        jnp.int32, (rows, rows), 1
+    )
+    unit = score_scale * LOG2E
+
+    def attend(n):
+        q = n // kv
+        j = n % kv
+
+        @pl.when(n < kv)
+        def _():
+            for load in kv_load(j):
+                load.wait()
+
+        lanes = pl.ds(pl.multiple_of(j * gw_cols, gw_cols), gw_cols)
+        block = q_ref[:, q, :, lanes].reshape(rows, gw_cols)
+        lhs = jnp.concatenate(
+            [block[:, g * HEAD_SIZE : (g + 1) * HEAD_SIZE] for g in range(group)], axis=0
+        )
+        row = base_row + q * RC
+        key = offset + lax.broadcasted_iota(jnp.int32, (group * rows, page_len - offset), 1)
+        tops, sums, outs = [], [], []
+        for p in range(pages):
+            reach, picks = facts[p]
+            bias = jnp.zeros((group * rows, 1), f32)
+            for t in range(tile_count):
+                inside = jnp.logical_and(row >= t * tile_rows, row < (t + 1) * tile_rows)
+                bias = jnp.where(inside, picks[t], bias)
+            scores = lax.dot_general(
+                lhs, k_buf[j, p], (((1,), (1,)), ((), ())), preferred_element_type=f32
+            )
+            late = jnp.where(key <= offset + row + reach, scores[:, offset:], masked_score)
+            scores = jnp.concatenate([scores[:, :offset], late], axis=1)
+            top = jnp.max(scores, axis=1, keepdims=True)
+            weights = jnp.exp2((scores - top) * unit)
+            sums.append(jnp.sum(weights, axis=1, keepdims=True))
+            outs.append(
+                jnp.dot(weights.astype(bf16), v_buf[j, p], preferred_element_type=f32)
+            )
+            tops.append(top * unit + bias)
+        best = functools.reduce(jnp.maximum, tops)
+        scales = [jnp.exp2(top - best) for top in tops]
+        total = sum(s * e for s, e in zip(sums, scales))
+        mixed = sum(o * (e / total) for o, e in zip(outs, scales))
+        lse = best + jnp.log2(total)
+        for g in range(group):
+            part_rows = slice(g * rows, (g + 1) * rows)
+            mix_out[n, :, :, g * HEAD_SIZE : (g + 1) * HEAD_SIZE] = (
+                mixed[part_rows].reshape(C, RC, HEAD_SIZE).astype(bf16)
+            )
+            lse_out[n, g : g + 1] = jnp.sum(
+                jnp.where(eye, lse[part_rows], 0.0), axis=0, keepdims=True
+            )
+        for copy in mix_sends(n):
+            copy.start()
+        mix_in[n, c] = mix_out[n, c]
+        lse_in[n, c] = lse_out[n]
+
+    def mix_sends(n):
+        copies = []
+        for d in range(1, C):
+            peer = (c + d) % C
+            copies.append(
+                remote(mix_out.at[n, peer], mix_in.at[n, c], mix_s.at[n, d], mix_r.at[n, c], peer, h)
+            )
+            copies.append(
+                remote(lse_out.at[n], lse_in.at[n, c], lse_s.at[n, d], lse_r.at[n, c], peer, h)
+            )
+        return copies
+
+    def att_sends(n):
+        copies = []
+        for d in range(1, C):
+            peer = (c + d) % C
+            copies.append(
+                remote(att.at[n, c], att.at[n, c], att_s.at[n, d], att_r.at[n, c], peer, h)
+            )
+        return copies
+
+    def combine(n):
+        for d in range(1, C):
+            peer = (c + C - d) % C
+            block = lse_in.at[n, peer]
+            remote(block, block, lse_s.at[n, d], lse_r.at[n, peer], peer, h).wait_recv()
+            block = mix_in.at[n, peer]
+            remote(block, block, mix_s.at[n, d], mix_r.at[n, peer], peer, h).wait_recv()
+        logs = [lse_in[n, k] for k in range(C)]
+        best = functools.reduce(jnp.maximum, logs)
+        scales = [jnp.exp2(value - best) for value in logs]
+        inverse = 1.0 / sum(scales)
+        lane = lax.broadcasted_iota(jnp.int32, (RC, rows), 1)
+        mine = lane == c * RC + lax.broadcasted_iota(jnp.int32, (RC, rows), 0)
+        for g in range(group):
+            cols = slice(g * HEAD_SIZE, (g + 1) * HEAD_SIZE)
+            value = jnp.zeros((RC, HEAD_SIZE), f32)
+            for k in range(C):
+                share = (scales[k] * inverse)[g : g + 1]
+                share = jnp.sum(jnp.where(mine, share, 0.0), axis=1, keepdims=True)
+                value = value + share * mix_in[n, k, :, cols].astype(f32)
+            att[n, c, :, cols] = value.astype(bf16)
+        for copy in att_sends(n):
+            copy.start()
+
+    def project(q):
+        for j in range(kv):
+            n = q * kv + j
+            for d in range(1, C):
+                peer = (c + C - d) % C
+                block = att.at[n, peer]
+                remote(block, block, att_s.at[n, d], att_r.at[n, peer], peer, h).wait_recv()
+        if q == 0:
+            loads[0].wait()
+        value = None
+        for j in range(kv):
+            term = lax.dot_general(
+                att[q * kv + j].reshape(rows, gw_cols),
+                ow[:, j * gw_cols : (j + 1) * gw_cols],
+                (((1,), (1,)), ((), ())),
+                preferred_element_type=f32,
+            )
+            value = term if value is None else value + term
+        po_out[q] = value.astype(bf16)
+        for i in range(NP):
+            piece = pl.ds(i * RP, RP)
+            send_if(
+                visitor,
+                po_out.at[q, piece],
+                po_in.at[q, h, piece],
+                po_s.at[q, i],
+                po_r.at[q, h, i],
+                c,
+                z,
+            )
+        po_in[q, h] = po_out[q]
+
+    def own(q, i):
+        if q == 0 and i == 0:
+            for d in range(1, H):
+                peer = (h + d) % H
+                block = res_in.at[peer]
+                remote(block, block, res_s.at[0], res_r.at[peer], c, peer).wait_recv()
+        for d in range(1, H):
+            peer = (h + d) % H
+            block = po_in.at[q, peer, pl.ds(i * RP, RP)]
+            remote(block, block, po_s.at[q, i], po_r.at[q, peer, i], c, peer).wait_recv()
+        spare = u.shape[-1] - width
+        lane = lax.broadcasted_iota(jnp.int32, (hr, spare), 1)
+        for b in range(i * RP // hr, (i + 1) * RP // hr):
+            span = slice(b * hr, (b + 1) * hr)
+            value = res_in[b, :, q].reshape(hr, width).astype(f32)
+            added = sum(po_in[q, k, span].astype(f32) for k in range(H))
+            stream = (value + added).astype(bf16)
+            st[q, span] = stream
+            stream = stream.astype(f32)
+            u[q, x, span, :width] = (stream * gain_ref[...]).astype(bf16)
+            squares = jnp.sum(stream * stream, axis=1, keepdims=True)
+            high = squares.astype(bf16).astype(f32)
+            mid = (squares - high).astype(bf16).astype(f32)
+            low = squares - high - mid
+            packed = jnp.where(lane == 0, high, jnp.where(lane == 1, mid, low))
+            packed = jnp.where(lane < 3, packed, 0.0)
+            u[q, x, span, width:] = packed.astype(bf16)
+
+    def relay(q, i):
+        piece = u.at[q, x, pl.ds(i * RP, RP)]
+        pl.when(visitor)(remote(piece, piece, u_s.at[q, i, 0], u_r.at[q, x, i], c, h).wait_recv)
+        up = jnp.logical_and(z >= h, z < Z - 1)
+        down = jnp.logical_and(z <= h, z > 0)
+        above = jnp.minimum(z + 1, Z - 1) * X + x
+        below = jnp.maximum(z - 1, 0) * X + x
+        send_if(up, piece, piece, u_s.at[q, i, 0], u_r.at[q, x, i], above, h)
+        send_if(down, piece, piece, u_s.at[q, i, 1], u_r.at[q, x, i], below, h)
+        for d in range(1, X):
+            peer = z * X + (x + d) % X
+            send(piece, piece, u_s.at[q, i, 1 + d], u_r.at[q, x, i], peer, h)
+
+    def spread(q):
+        for i in range(NP):
+            pl.when(owner)(functools.partial(own, q, i))
+            relay(q, i)
+
+    def gather(q):
+        for d in range(1, X):
+            source = (x + d) % X
+            for i in range(NP):
+                block = u.at[q, source, pl.ds(i * RP, RP)]
+                remote(block, block, u_s.at[q, i, 1 + d], u_r.at[q, source, i], c, h).wait_recv()
+        if q == 0:
+            loads[1].wait()
+            loads[2].wait()
+        squares = 0.0
+        for k in range(X):
+            split = u[q, k, :, width:].astype(f32)
+            squares = squares + jnp.sum(split, axis=1, keepdims=True)
+        squares = jnp.broadcast_to(squares, (rows, 128)).reshape(Y, CORES, hr, 128)
+        ss_out[q] = squares.swapaxes(0, 1)
+        send(ss_out.at[q, CORES - 1 - core], ss_in.at[q], ss_s.at[q, 0], ss_r.at[q, 0], c, partner)
+
+    def matmul(q, i, which):
+        weight = (gw, uw)[which]
+        cols = slice(i * tile, (i + 1) * tile)
+        value = None
+        for k in range(X):
+            term = jnp.dot(
+                u[q, k, :, :width],
+                weight[k * width : (k + 1) * width, cols],
+                preferred_element_type=f32,
+            )
+            value = term if value is None else value + term
+        value = value.reshape(Y, CORES, hr, tile).swapaxes(0, 1).astype(bf16)
+        first[q, i, which] = value
+        send(
+            first.at[q, i, which, CORES - 1 - core],
+            first_in.at[q, i, which],
+            f_s.at[q, i, which],
+            f_r.at[q, i, which],
+            c,
+            partner,
+        )
+
+    def middle(q, i, which):
+        block = first_in.at[q, i, which]
+        remote(block, block, f_s.at[q, i, which], f_r.at[q, i, which], c, partner).wait_recv()
+        both = first[q, i, which, core].astype(f32) + first_in[q, i, which].astype(f32)
+        second[q, i, which] = both.astype(bf16)
+        for d in range(1, Y):
+            peer = (y + d) % Y
+            send(
+                second.at[q, i, which, peer],
+                second_in.at[q, i, which, y],
+                g_s.at[q, i, which, d],
+                g_r.at[q, i, which, y],
+                c,
+                peer * CORES + core,
+            )
+
+    def middle_squares(q):
+        block = ss_in.at[q]
+        remote(block, block, ss_s.at[q, 0], ss_r.at[q, 0], c, partner).wait_recv()
+        ss_mid[q] = ss_out[q, core] + ss_in[q]
+        for d in range(1, Y):
+            peer = (y + d) % Y
+            send(
+                ss_mid.at[q, peer],
+                ss_last.at[q, y],
+                ss_s.at[q, d],
+                ss_r.at[q, 1 + y],
+                c,
+                peer * CORES + core,
+            )
+
+    def inverse_rms(q):
+        total = ss_mid[q, y]
+        for d in range(1, Y):
+            peer = (y + Y - d) % Y
+            block = ss_last.at[q, peer]
+            remote(
+                block, block, ss_s.at[q, d], ss_r.at[q, 1 + peer], c, peer * CORES + core
+            ).wait_recv()
+            total = total + ss_last[q, peer]
+        return lax.rsqrt(total[:, :1] / (C * width) + norm_epsilon)
+
+    def finish(q, i, inverse):
+        sums = []
+        for which in range(2):
+            value = second[q, i, which, y].astype(f32)
+            for d in range(1, Y):
+                peer = (y + Y - d) % Y
+                block = second_in.at[q, i, which, peer]
+                remote(
+                    block,
+                    block,
+                    g_s.at[q, i, which, d],
+                    g_r.at[q, i, which, peer],
+                    c,
+                    peer * CORES + core,
+                ).wait_recv()
+                value = value + second_in[q, i, which, peer].astype(f32)
+            sums.append(value * inverse)
+        hid[q, i, h] = (jax.nn.gelu(sums[0], approximate=True) * sums[1]).astype(bf16)
+        block = hid.at[q, i, h]
+        for d in range(1, Y):
+            peer = ((y + d) % Y) * CORES + core
+            send(block, block, h_s.at[q, i, d], h_r.at[q, i, h], c, peer)
+        send(block, block, h_s.at[q, i, 0], h_r.at[q, i, h], c, partner)
+
+    def forward(q, i):
+        for d in range(1, Y):
+            origin = ((y + Y - d) % Y) * CORES + core
+            block = hid.at[q, i, origin]
+            remote(block, block, h_s.at[q, i, d], h_r.at[q, i, origin], c, origin).wait_recv()
+            send(block, block, fw_s.at[q, i, d], h_r.at[q, i, origin], c, partner)
+
+    def down(q, i):
+        for d in range(Y):
+            origin = ((y + Y - d) % Y) * CORES + (CORES - 1 - core)
+            block = hid.at[q, i, origin]
+            remote(block, block, h_s.at[q, i, 0], h_r.at[q, i, origin], c, partner).wait_recv()
+        if q == 0 and i == 0:
+            loads[3].wait()
+        term = lax.dot_general(
+            hid[q, i].reshape(rows, tile),
+            dw[:, i * tile : (i + 1) * tile],
+            (((1,), (1,)), ((), ())),
+            preferred_element_type=f32,
+        )
+        if i == 0:
+            acc[...] = term
+        else:
+            acc[...] += term
+
+    def scatter(q):
+        for k in range(X):
+
+            @pl.when(jnp.logical_and(owner, x == k))
+            def _(k=k):
+                acc[:, k * width : (k + 1) * width] += st[q].astype(f32)
+
+        part[q] = acc[...].reshape(C, RC, acc.shape[1]).astype(bf16)
+        for d in range(1, C):
+            peer = (c + d) % C
+            send(part.at[q, peer], part_in.at[q, c], part_s.at[q, d], part_r.at[q, c], peer, h)
+        part_in[q, c] = part[q, c]
+
+    def collect(q):
+        for d in range(1, C):
+            peer = (c + C - d) % C
+            block = part_in.at[q, peer]
+            remote(block, block, part_s.at[q, d], part_r.at[q, peer], peer, h).wait_recv()
+        out_ref[q] = sum(part_in[q, k].astype(f32) for k in range(C)).astype(bf16)
+
+    steps = NQ * kv
+    lag = 2
+
+    def loop(n, carry):
+        attend(n)
+
+        @pl.when(n >= lag)
+        def _():
+            combine(n - lag)
+
+        return carry
+
+    lax.fori_loop(0, steps, loop, 0)
+    project(0)
+    for n in range(steps - lag, steps):
+        combine(n)
+
+    pairs = [(i, which) for i in range(tiles) for which in range(2)]
+
+    def expand(q):
+        gather(q)
+        for n, (i, which) in enumerate(pairs):
+            matmul(q, i, which)
+            if n == 1:
+                middle_squares(q)
+            if n:
+                middle(q, *pairs[n - 1])
+        middle(q, *pairs[-1])
+
+    def contract(q):
+        inverse = inverse_rms(q)
+        for i in range(tiles):
+            finish(q, i, inverse)
+            if i:
+                forward(q, i - 1)
+        forward(q, tiles - 1)
+
+    spread(0)
+    for q in range(1, NQ):
+        project(q)
+    for q in range(NQ):
+        expand(q)
+        if q + 1 < NQ:
+            spread(q + 1)
+        contract(q)
+        for i in range(tiles):
+            down(q, i)
+        scatter(q)
+    for q in range(NQ):
+        collect(q)
+
+    def drain(n, carry):
+        for copy in mix_sends(n) + att_sends(n):
+            copy.wait_send()
+        return carry
+
+    lax.fori_loop(0, steps, drain, 0)
+    for copy in sent:
+        copy.wait_send()
+    for condition, copy in kept:
+        pl.when(condition)(copy.wait_send)
+
+
+def fused(
+    C,
+    H,
+    queries,
+    keys,
+    values,
+    page_map,
+    selected,
+    residual_in,
+    out_weight,
+    norm_gain,
+    gate_weight,
+    up_weight,
+    down_weight,
+):
+    row_count, query_width = queries.shape
+    pages, page_len, kv_width = keys.shape
+    kv = kv_width // HEAD_SIZE
+    group = query_width // kv_width
+    NQ = row_count // 128
+    RC = row_count // C // NQ
+    rows = C * RC
+    NP = 2
+    X = C // H
+    Y = H // CORES
+    hr = rows // H
+    width = out_weight.shape[1]
+    hidden = gate_weight.shape[1]
+    out_width = down_weight.shape[1]
+    tile = column_tile(hidden)
+    tiles = hidden // tile
+    steps = NQ * kv
+    u_width = (width + 127) // 128 * 128
+    bf16 = jnp.bfloat16
+    f32 = jnp.float32
+    vmem = pl.BlockSpec(memory_space=pltpu.VMEM)
+    smem = pl.BlockSpec(memory_space=pltpu.SMEM)
+    hbm = pl.BlockSpec(memory_space=pl.ANY)
+    V = pltpu.VMEM
+    S = pltpu.SemaphoreType.DMA
+    out_weight = out_weight.T
+    down_weight = down_weight.T
+    mixes = V((steps, C, RC, group * HEAD_SIZE), bf16)
+    return pl.pallas_call(
+        functools.partial(fused_kernel, C, H, NP),
+        out_shape=jax.ShapeDtypeStruct((NQ, RC, out_width), bf16),
+        in_specs=[smem] * 2 + [vmem] * 3 + [hbm] * 6,
+        out_specs=vmem,
+        scratch_shapes=[
+            V((kv, pages, page_len, HEAD_SIZE), bf16),
+            V((kv, pages, page_len, HEAD_SIZE), bf16),
+            V(out_weight.shape, bf16),
+            V(gate_weight.shape, bf16),
+            V(up_weight.shape, bf16),
+            V(down_weight.shape, bf16),
+            mixes,
+            mixes,
+            V((steps, group, rows), f32),
+            V((steps, C, group, rows), f32),
+            mixes,
+            V((NQ, rows, width), bf16),
+            V((NQ, H, rows, width), bf16),
+            V((H, X, NQ, RC, width), bf16),
+            V((NQ, rows, width), bf16),
+            V((NQ, X, rows, u_width), bf16),
+            V((NQ, CORES, Y, hr, 128), f32),
+            V((NQ, Y, hr, 128), f32),
+            V((NQ, Y, hr, 128), f32),
+            V((NQ, Y, hr, 128), f32),
+            V((NQ, tiles, 2, CORES, Y, hr, tile), bf16),
+            V((NQ, tiles, 2, Y, hr, tile), bf16),
+            V((NQ, tiles, 2, Y, hr, tile), bf16),
+            V((NQ, tiles, 2, Y, hr, tile), bf16),
+            V((NQ, tiles, H, hr, tile), bf16),
+            V((rows, out_width), f32),
+            V((NQ, C, RC, out_width), bf16),
+            V((NQ, C, RC, out_width), bf16),
+            S((2, kv)),
+            S((4,)),
+            S((steps, C)),
+            S((steps, C)),
+            S((steps, C)),
+            S((steps, C)),
+            S((steps, C)),
+            S((steps, C)),
+            S((NQ, NP)),
+            S((NQ, H, NP)),
+            S((1,)),
+            S((H,)),
+            S((NQ, NP, 1 + X)),
+            S((NQ, X, NP)),
+            S((NQ, Y)),
+            S((NQ, 1 + Y)),
+            S((NQ, tiles, 2)),
+            S((NQ, tiles, 2)),
+            S((NQ, tiles, 2, Y)),
+            S((NQ, tiles, 2, Y)),
+            S((NQ, tiles, Y)),
+            S((NQ, tiles, H)),
+            S((NQ, tiles, Y)),
+            S((NQ, C)),
+            S((NQ, C)),
+        ],
+        compiler_params=pltpu.CompilerParams(
+            has_side_effects=True, vmem_limit_bytes=63 * 2**20
+        ),
+    )(
+        page_map,
+        selected,
+        queries.reshape(C, NQ, RC, query_width),
+        residual_in.reshape(X, NQ, RC, width),
+        norm_gain.reshape(1, width),
+        keys,
+        values,
+        out_weight,
+        gate_weight,
+        up_weight,
+        down_weight,
+    ).reshape(row_count // C, out_width)
+
+
+def fits(C, H, queries, keys, selected, out_weight, gate_weight):
+    rows = queries.shape[0]
+    width = out_weight.shape[1]
+    if rows % 128:
+        return False
+    chunks = rows // 128
+    return (
+        C % H == 0
+        and (C // H) * H == C
+        and rows % (C * chunks) == 0
+        and rows // (C * chunks) % 16 == 0
+        and rows % selected.shape[0] == 0
+        and (keys.shape[1] - rows) % 128 == 0
+        and keys.shape[1] > rows
+        and width % 16 == 0
+        and width % 128 <= 125
+        and width % 128 > 0
+        and gate_weight.shape[1] % 128 == 0
+    )
+
+
 def shards(
     queries,
     keys,
@@ -557,6 +1258,22 @@
     ctx_index = lax.axis_index("ctx")
     C = lax.axis_size("ctx")
     H = lax.axis_size("head")
+    if fits(C, H, queries, keys, selected, out_weight, gate_weight):
+        return fused(
+            C,
+            H,
+            queries,
+            keys,
+            values,
+            page_map,
+            selected,
+            residual_in,
+            out_weight,
+            norm_gain,
+            gate_weight,
+            up_weight,
+            down_weight,
+        )
     row_max, row_total, mixture = owner_pass(
         queries, keys, values, page_map, selected, ctx_index, C
     )

time: 144 us -> 108 us (0.75)
  the two profiles are of different devices: /device:TPU:22 before, /device:TPU:0 now
where the time goes in v2:
time: 108 us
  Pallas kernels  105 us (97%)
  local copies, waits for them, and re-layouts  2.8 us (3%)
    pallas_call x1, Pallas kernels, fused(): pl.pallas_call(functools.partial(fused_kernel, C, H, NP), out_shape=jax.S...  105 us

profile of v2, /device:TPU:0, one launch (start us, length us, event | category | flops | bytes accessed | tf_op | source)
XLA Modules:
  0.0 108.0 jit_solution(3412428784151888295)
XLA Ops:
  0.0 1.3 %reshape.14.gain_ref = f32[1,672]{1,0:T(1,128)} reshape(f32[672]{0:T(1024)} %param.18) | data formatting | bytes 5376 | tf_op jit(solution)/shard_map/reshape | solution.py:1214
  1.3 105.1 %shard_map.109 = bf16[2,16,1344]{2,1,0:T(8,128)(2,1)} custom-call(s32[16]{0:T(128)} %map_ref.1, s32[2,8]{1,0:T(2,128)} %sel_ref.1, bf16[8,2,16,1024]{3,2,1,0:T(8,128)(2,1)} %bitcast.7, bf16[2,2,16,672]{3,2,1,0:T(8,128)(2,1)} %bitcast.9, f32[1,672]{1,0:T(1,128)} %reshape.14.gain_ref, bf16[2,2048,512]{2,1,0:T(8,128)(2,1)} %k_hbm.1, ...), custom_call_target="tpu_custom_call" | custom-call | tf_op jit(solution)/shard_map/pallas_call | solution.py:1146
  106.4 1.5 %copy.13 = bf16[32,1344]{1,0:T(8,128)(2,1)} copy(bf16[32,1344]{1,0:T(8,128)(2,1)} %bitcast.8) | data formatting | bytes 172032

commit v3 on v2

--- a/solution.py
+++ b/solution.py
@@ -548,11 +548,11 @@
     C,
     H,
     NP,
-    map_ref,
-    sel_ref,
-    q_ref,
-    res_ref,
-    gain_ref,
+    map_hbm,
+    sel_hbm,
+    q_hbm,
+    res_hbm,
+    gain_hbm,
     k_hbm,
     v_hbm,
     ow_hbm,
@@ -560,6 +560,11 @@
     uw_hbm,
     dw_hbm,
     out_ref,
+    map_ref,
+    sel_ref,
+    q_ref,
+    res_ref,
+    gain_ref,
     k_buf,
     v_buf,
     ow,
@@ -588,6 +593,7 @@
     acc,
     part,
     part_in,
+    in_sem,
     kv_sem,
     w_sem,
     mix_s,
@@ -610,7 +616,6 @@
     g_r,
     h_s,
     h_r,
-    fw_s,
     part_s,
     part_r,
 ):
@@ -656,6 +661,9 @@
     sent = []
     kept = []
 
+    def start(*args):
+        remote(*args).start()
+
     def send(*args):
         copy = remote(*args)
         copy.start()
@@ -673,6 +681,29 @@
             pltpu.make_async_copy(v_hbm.at[:, :, lanes], v_buf.at[j], kv_sem.at[1, j]),
         )
 
+    barrier = pltpu.get_barrier_semaphore()
+    for d in range(1, C):
+        pl.semaphore_signal(
+            barrier, inc=1, device_id=((c + d) % C, h), device_id_type=MESH
+        )
+    for d in range(1, H):
+        pl.semaphore_signal(
+            barrier, inc=1, device_id=(c, (h + d) % H), device_id_type=MESH
+        )
+    inputs = [
+        pltpu.make_async_copy(src, dst, in_sem.at[i])
+        for i, (src, dst) in enumerate(
+            (
+                (map_hbm, map_ref),
+                (sel_hbm, sel_ref),
+                (q_hbm, q_ref),
+                (res_hbm, res_ref),
+                (gain_hbm, gain_ref.at[0]),
+            )
+        )
+    ]
+    for load in inputs:
+        load.start()
     for j in range(kv):
         for load in kv_load(j):
             load.start()
@@ -682,11 +713,8 @@
             ((ow_hbm, ow), (gw_hbm, gw), (uw_hbm, uw), (dw_hbm, dw))
         )
     ]
-    for load in loads:
-        load.start()
-
-    send_if(visitor, res_ref, res_in.at[h], res_s.at[0], res_r.at[h], c, z)
-    res_in[h] = res_ref[...]
+    for load in inputs:
+        load.wait()
 
     facts = []
     for p in range(pages):
@@ -719,6 +747,11 @@
         def _():
             for load in kv_load(j):
                 load.wait()
+
+        @pl.when(n == 0)
+        def _():
+            for load in loads:
+                load.start()
 
         lanes = pl.ds(pl.multiple_of(j * gw_cols, gw_cols), gw_cols)
         block = q_ref[:, q, :, lanes].reshape(rows, gw_cols)
@@ -759,39 +792,29 @@
             lse_out[n, g : g + 1] = jnp.sum(
                 jnp.where(eye, lse[part_rows], 0.0), axis=0, keepdims=True
             )
-        for copy in mix_sends(n):
-            copy.start()
         mix_in[n, c] = mix_out[n, c]
         lse_in[n, c] = lse_out[n]
 
     def mix_sends(n):
-        copies = []
         for d in range(1, C):
             peer = (c + d) % C
-            copies.append(
-                remote(mix_out.at[n, peer], mix_in.at[n, c], mix_s.at[n, d], mix_r.at[n, c], peer, h)
-            )
-            copies.append(
-                remote(lse_out.at[n], lse_in.at[n, c], lse_s.at[n, d], lse_r.at[n, c], peer, h)
-            )
-        return copies
+            remote(mix_out.at[n, peer], mix_in.at[n, c], mix_s.at[0], mix_r.at[n], peer, h).start()
+            remote(lse_out.at[n], lse_in.at[n, c], lse_s.at[0], lse_r.at[n], peer, h).start()
 
     def att_sends(n):
-        copies = []
         for d in range(1, C):
             peer = (c + d) % C
-            copies.append(
-                remote(att.at[n, c], att.at[n, c], att_s.at[n, d], att_r.at[n, c], peer, h)
-            )
-        return copies
+            remote(att.at[n, c], att.at[n, c], att_s.at[0], att_r.at[n], peer, h).start()
+
+    def arrived(block, recv_sem):
+        remote(block, block, recv_sem, recv_sem, c, partner).wait_recv()
+
+    def left(block, send_sem):
+        remote(block, block, send_sem, send_sem, c, partner).wait_send()
 
     def combine(n):
-        for d in range(1, C):
-            peer = (c + C - d) % C
-            block = lse_in.at[n, peer]
-            remote(block, block, lse_s.at[n, d], lse_r.at[n, peer], peer, h).wait_recv()
-            block = mix_in.at[n, peer]
-            remote(block, block, mix_s.at[n, d], mix_r.at[n, peer], peer, h).wait_recv()
+        arrived(lse_in.at[n, pl.ds(0, C - 1)], lse_r.at[n])
+        arrived(mix_in.at[n, pl.ds(0, C - 1)], mix_r.at[n])
         logs = [lse_in[n, k] for k in range(C)]
         best = functools.reduce(jnp.maximum, logs)
         scales = [jnp.exp2(value - best) for value in logs]
@@ -806,16 +829,12 @@
                 share = jnp.sum(jnp.where(mine, share, 0.0), axis=1, keepdims=True)
                 value = value + share * mix_in[n, k, :, cols].astype(f32)
             att[n, c, :, cols] = value.astype(bf16)
-        for copy in att_sends(n):
-            copy.start()
+        att_sends(n)
 
     def project(q):
         for j in range(kv):
             n = q * kv + j
-            for d in range(1, C):
-                peer = (c + C - d) % C
-                block = att.at[n, peer]
-                remote(block, block, att_s.at[n, d], att_r.at[n, peer], peer, h).wait_recv()
+            arrived(att.at[n, pl.ds(0, C - 1)], att_r.at[n])
         if q == 0:
             loads[0].wait()
         value = None
@@ -830,27 +849,16 @@
         po_out[q] = value.astype(bf16)
         for i in range(NP):
             piece = pl.ds(i * RP, RP)
-            send_if(
-                visitor,
-                po_out.at[q, piece],
-                po_in.at[q, h, piece],
-                po_s.at[q, i],
-                po_r.at[q, h, i],
-                c,
-                z,
+            copy = remote(
+                po_out.at[q, piece], po_in.at[q, h, piece], po_s.at[q], po_r.at[q, i], c, z
             )
+            pl.when(visitor)(copy.start)
         po_in[q, h] = po_out[q]
 
     def own(q, i):
         if q == 0 and i == 0:
-            for d in range(1, H):
-                peer = (h + d) % H
-                block = res_in.at[peer]
-                remote(block, block, res_s.at[0], res_r.at[peer], c, peer).wait_recv()
-        for d in range(1, H):
-            peer = (h + d) % H
-            block = po_in.at[q, peer, pl.ds(i * RP, RP)]
-            remote(block, block, po_s.at[q, i], po_r.at[q, peer, i], c, peer).wait_recv()
+            arrived(res_in.at[pl.ds(0, H - 1)], res_r.at[0])
+        arrived(po_in.at[q, pl.ds(0, H - 1), pl.ds(i * RP, RP)], po_r.at[q, i])
         spare = u.shape[-1] - width
         lane = lax.broadcasted_iota(jnp.int32, (hr, spare), 1)
         for b in range(i * RP // hr, (i + 1) * RP // hr):
@@ -869,30 +877,31 @@
             packed = jnp.where(lane < 3, packed, 0.0)
             u[q, x, span, width:] = packed.astype(bf16)
 
-    def relay(q, i):
+    def relay(q, i, here):
         piece = u.at[q, x, pl.ds(i * RP, RP)]
-        pl.when(visitor)(remote(piece, piece, u_s.at[q, i, 0], u_r.at[q, x, i], c, h).wait_recv)
-        up = jnp.logical_and(z >= h, z < Z - 1)
-        down = jnp.logical_and(z <= h, z > 0)
+        recv = u_r.at[q, x, i]
+        pl.when(jnp.logical_and(here, visitor))(functools.partial(arrived, piece, recv))
+        up = jnp.logical_and(here, jnp.logical_and(z >= h, z < Z - 1))
+        down = jnp.logical_and(here, jnp.logical_and(z <= h, z > 0))
         above = jnp.minimum(z + 1, Z - 1) * X + x
         below = jnp.maximum(z - 1, 0) * X + x
-        send_if(up, piece, piece, u_s.at[q, i, 0], u_r.at[q, x, i], above, h)
-        send_if(down, piece, piece, u_s.at[q, i, 1], u_r.at[q, x, i], below, h)
+        send_if(up, piece, piece, u_s.at[q, i, 0], recv, above, h)
+        send_if(down, piece, piece, u_s.at[q, i, 1], recv, below, h)
         for d in range(1, X):
             peer = z * X + (x + d) % X
-            send(piece, piece, u_s.at[q, i, 1 + d], u_r.at[q, x, i], peer, h)
-
-    def spread(q):
+            send_if(here, piece, piece, u_s.at[q, i, 1 + d], recv, peer, h)
+
+    def spread(q, here):
         for i in range(NP):
-            pl.when(owner)(functools.partial(own, q, i))
-            relay(q, i)
+            pl.when(jnp.logical_and(here, owner))(functools.partial(own, q, i))
+            relay(q, i, here)
 
     def gather(q):
         for d in range(1, X):
             source = (x + d) % X
             for i in range(NP):
                 block = u.at[q, source, pl.ds(i * RP, RP)]
-                remote(block, block, u_s.at[q, i, 1 + d], u_r.at[q, source, i], c, h).wait_recv()
+                arrived(block, u_r.at[q, source, i])
         if q == 0:
             loads[1].wait()
             loads[2].wait()
@@ -917,10 +926,10 @@
             value = term if value is None else value + term
         value = value.reshape(Y, CORES, hr, tile).swapaxes(0, 1).astype(bf16)
         first[q, i, which] = value
-        send(
+        start(
             first.at[q, i, which, CORES - 1 - core],
             first_in.at[q, i, which],
-            f_s.at[q, i, which],
+            f_s.at[0],
             f_r.at[q, i, which],
             c,
             partner,
@@ -928,15 +937,15 @@
 
     def middle(q, i, which):
         block = first_in.at[q, i, which]
-        remote(block, block, f_s.at[q, i, which], f_r.at[q, i, which], c, partner).wait_recv()
+        arrived(block, f_r.at[q, i, which])
         both = first[q, i, which, core].astype(f32) + first_in[q, i, which].astype(f32)
         second[q, i, which] = both.astype(bf16)
         for d in range(1, Y):
             peer = (y + d) % Y
-            send(
+            start(
                 second.at[q, i, which, peer],
                 second_in.at[q, i, which, y],
-                g_s.at[q, i, which, d],
+                g_s.at[0],
                 g_r.at[q, i, which, y],
                 c,
                 peer * CORES + core,
@@ -978,7 +987,7 @@
                 remote(
                     block,
                     block,
-                    g_s.at[q, i, which, d],
+                    g_s.at[0],
                     g_r.at[q, i, which, peer],
                     c,
                     peer * CORES + core,
@@ -989,21 +998,21 @@
         block = hid.at[q, i, h]
         for d in range(1, Y):
             peer = ((y + d) % Y) * CORES + core
-            send(block, block, h_s.at[q, i, d], h_r.at[q, i, h], c, peer)
-        send(block, block, h_s.at[q, i, 0], h_r.at[q, i, h], c, partner)
+            start(block, block, h_s.at[0], h_r.at[q, i, h], c, peer)
+        start(block, block, h_s.at[0], h_r.at[q, i, h], c, partner)
 
     def forward(q, i):
         for d in range(1, Y):
             origin = ((y + Y - d) % Y) * CORES + core
             block = hid.at[q, i, origin]
-            remote(block, block, h_s.at[q, i, d], h_r.at[q, i, origin], c, origin).wait_recv()
-            send(block, block, fw_s.at[q, i, d], h_r.at[q, i, origin], c, partner)
+            arrived(block, h_r.at[q, i, origin])
+            start(block, block, h_s.at[0], h_r.at[q, i, origin], c, partner)
 
     def down(q, i):
         for d in range(Y):
             origin = ((y + Y - d) % Y) * CORES + (CORES - 1 - core)
             block = hid.at[q, i, origin]
-            remote(block, block, h_s.at[q, i, 0], h_r.at[q, i, origin], c, partner).wait_recv()
+            arrived(block, h_r.at[q, i, origin])
         if q == 0 and i == 0:
             loads[3].wait()
         term = lax.dot_general(
@@ -1027,31 +1036,38 @@
         part[q] = acc[...].reshape(C, RC, acc.shape[1]).astype(bf16)
         for d in range(1, C):
             peer = (c + d) % C
-            send(part.at[q, peer], part_in.at[q, c], part_s.at[q, d], part_r.at[q, c], peer, h)
+            start(part.at[q, peer], part_in.at[q, c], part_s.at[0], part_r.at[q], peer, h)
         part_in[q, c] = part[q, c]
 
     def collect(q):
-        for d in range(1, C):
-            peer = (c + C - d) % C
-            block = part_in.at[q, peer]
-            remote(block, block, part_s.at[q, d], part_r.at[q, peer], peer, h).wait_recv()
+        arrived(part_in.at[q, pl.ds(0, C - 1)], part_r.at[q])
         out_ref[q] = sum(part_in[q, k].astype(f32) for k in range(C)).astype(bf16)
 
+    pl.semaphore_wait(barrier, C + H - 2)
+    send_if(visitor, res_ref, res_in.at[h], res_s.at[0], res_r.at[0], c, z)
+    res_in[h] = res_ref[...]
+
     steps = NQ * kv
-    lag = 2
+    lag = 3
 
     def loop(n, carry):
         attend(n)
-
-        @pl.when(n >= lag)
+        pl.when(jnp.logical_or(n < kv, n >= kv + lag))(functools.partial(mix_sends, n))
+
+        @pl.when(jnp.logical_and(n >= lag, n < kv + lag))
         def _():
             combine(n - lag)
 
+        @pl.when(n == kv + lag - 1)
+        def _():
+            for k in range(kv, kv + lag):
+                mix_sends(k)
+
         return carry
 
     lax.fori_loop(0, steps, loop, 0)
     project(0)
-    for n in range(steps - lag, steps):
+    for n in range(kv, steps):
         combine(n)
 
     pairs = [(i, which) for i in range(tiles) for which in range(2)]
@@ -1074,13 +1090,15 @@
                 forward(q, i - 1)
         forward(q, tiles - 1)
 
-    spread(0)
-    for q in range(1, NQ):
-        project(q)
+    near = jnp.logical_and(z - h <= 1, h - z <= 1)
+    always = z >= 0
+    spread(0, near)
+    project(1)
+    spread(0, jnp.logical_not(near))
+    expand(0)
+    spread(1, always)
+    expand(1)
     for q in range(NQ):
-        expand(q)
-        if q + 1 < NQ:
-            spread(q + 1)
         contract(q)
         for i in range(tiles):
             down(q, i)
@@ -1088,12 +1106,15 @@
     for q in range(NQ):
         collect(q)
 
-    def drain(n, carry):
-        for copy in mix_sends(n) + att_sends(n):
-            copy.wait_send()
-        return carry
-
-    lax.fori_loop(0, steps, drain, 0)
+    left(mix_out.at[:, pl.ds(0, C - 1)], mix_s.at[0])
+    left(lse_in.at[:, pl.ds(0, C - 1)], lse_s.at[0])
+    left(att.at[:, pl.ds(0, C - 1)], att_s.at[0])
+    left(first_in, f_s.at[0])
+    left(second.at[:, :, :, pl.ds(0, Y - 1)], g_s.at[0])
+    left(hid.at[:, :, pl.ds(0, 2 * Y - 1)], h_s.at[0])
+    left(part.at[:, pl.ds(0, C - 1)], part_s.at[0])
+    for q in range(NQ):
+        pl.when(visitor)(functools.partial(left, po_out.at[q], po_s.at[q]))
     for copy in sent:
         copy.wait_send()
     for condition, copy in kept:
@@ -1136,7 +1157,6 @@
     bf16 = jnp.bfloat16
     f32 = jnp.float32
     vmem = pl.BlockSpec(memory_space=pltpu.VMEM)
-    smem = pl.BlockSpec(memory_space=pltpu.SMEM)
     hbm = pl.BlockSpec(memory_space=pl.ANY)
     V = pltpu.VMEM
     S = pltpu.SemaphoreType.DMA
@@ -1146,9 +1166,14 @@
     return pl.pallas_call(
         functools.partial(fused_kernel, C, H, NP),
         out_shape=jax.ShapeDtypeStruct((NQ, RC, out_width), bf16),
-        in_specs=[smem] * 2 + [vmem] * 3 + [hbm] * 6,
+        in_specs=[hbm] * 11,
         out_specs=vmem,
         scratch_shapes=[
+            pltpu.SMEM(page_map.shape, jnp.int32),
+            pltpu.SMEM(selected.shape, jnp.int32),
+            V((C, NQ, RC, query_width), bf16),
+            V((X, NQ, RC, width), bf16),
+            V((1, width), f32),
             V((kv, pages, page_len, HEAD_SIZE), bf16),
             V((kv, pages, page_len, HEAD_SIZE), bf16),
             V(out_weight.shape, bf16),
@@ -1177,41 +1202,41 @@
             V((rows, out_width), f32),
             V((NQ, C, RC, out_width), bf16),
             V((NQ, C, RC, out_width), bf16),
+            S((5,)),
             S((2, kv)),
             S((4,)),
-            S((steps, C)),
-            S((steps, C)),
-            S((steps, C)),
-            S((steps, C)),
-            S((steps, C)),
-            S((steps, C)),
+            S((1,)),
+            S((steps,)),
+            S((1,)),
+            S((steps,)),
+            S((1,)),
+            S((steps,)),
+            S((NQ,)),
             S((NQ, NP)),
-            S((NQ, H, NP)),
             S((1,)),
-            S((H,)),
+            S((1,)),
             S((NQ, NP, 1 + X)),
             S((NQ, X, NP)),
             S((NQ, Y)),
             S((NQ, 1 + Y)),
+            S((1,)),
             S((NQ, tiles, 2)),
-            S((NQ, tiles, 2)),
+            S((1,)),
             S((NQ, tiles, 2, Y)),
-            S((NQ, tiles, 2, Y)),
-            S((NQ, tiles, Y)),
+            S((1,)),
             S((NQ, tiles, H)),
-            S((NQ, tiles, Y)),
-            S((NQ, C)),
-            S((NQ, C)),
+            S((1,)),
+            S((NQ,)),
         ],
         compiler_params=pltpu.CompilerParams(
-            has_side_effects=True, vmem_limit_bytes=63 * 2**20
+            collective_id=0, has_side_effects=True, vmem_limit_bytes=63 * 2**20
         ),
     )(
         page_map,
         selected,
         queries.reshape(C, NQ, RC, query_width),
         residual_in.reshape(X, NQ, RC, width),
-        norm_gain.reshape(1, width),
+        norm_gain,
         keys,
         values,
         out_weight,
@@ -1228,11 +1253,13 @@
         return False
     chunks = rows // 128
     return (
-        C % H == 0
+        chunks == 2
+        and C % H == 0
         and (C // H) * H == C
         and rows % (C * chunks) == 0
         and rows // (C * chunks) % 16 == 0
         and rows % selected.shape[0] == 0
+        and keys.shape[2] // HEAD_SIZE > 3
         and (keys.shape[1] - rows) % 128 == 0
         and keys.shape[1] > rows
         and width % 16 == 0

time: 108 us -> 98.8 us (0.915)
  Pallas kernels: 105 us -> 97.1 us
  local copies, waits for them, and re-layouts: 2.8 us -> 1.54 us
    pallas_call x1, Pallas kernels: 105 us -> 97.1 us  [fused(): pl.pallas_call(functools.partial(fused_kernel, C, H, NP), out_shape=jax.S...]
    reshape x1 -> x0, local copies, waits for them, and re-layouts: 1.27 us -> none  [fused(): norm_gain.reshape(1, width)]
where the time goes in v3:
time: 98.8 us; the launch traced here: 98.7 us
  Pallas kernels  97.1 us (98%)
  local copies, waits for them, and re-layouts  1.54 us (2%)
    pallas_call x1, Pallas kernels, fused(): pl.pallas_call(functools.partial(fused_kernel, C, H, NP), out_shape=jax.S...  97.1 us

profile of v3, /device:TPU:0, one launch (start us, length us, event | category | flops | bytes accessed | tf_op | source)
XLA Modules:
  0.0 98.7 jit_solution(9626403387603957283)
XLA Ops:
  0.0 97.1 %shard_map.109 = bf16[2,16,1344]{2,1,0:T(8,128)(2,1)} custom-call(s32[16]{0:T(128)} %map_hbm.1, s32[2,8]{1,0:T(2,128)} %sel_hbm.1, bf16[8,2,16,1024]{3,2,1,0:T(8,128)(2,1)} %bitcast.7, bf16[2,2,16,672]{3,2,1,0:T(8,128)(2,1)} %bitcast.9, f32[672]{0:T(1024)} %gain_hbm.1, bf16[2,2048,512]{2,1,0:T(8,128)(2,1)} %k_hbm.1, bf16[2,2048,512]{2,1,0:T(8,128)(2,1)} %v_hbm.1, ...), custom_call_target="tpu_custom_call" | custom-call | tf_op jit(solution)/shard_map/pallas_call | solution.py:1166
  97.1 1.5 %copy.13 = bf16[32,1344]{1,0:T(8,128)(2,1)} copy(bf16[32,1344]{1,0:T(8,128)(2,1)} %bitcast.8) | data formatting | bytes 172032

commit v4 on v3

--- a/solution.py
+++ b/solution.py
@@ -585,6 +585,7 @@
     ss_in,
     ss_mid,
     ss_last,
+    scale,
     first,
     first_in,
     second,
@@ -975,9 +976,10 @@
                 block, block, ss_s.at[q, d], ss_r.at[q, 1 + peer], c, peer * CORES + core
             ).wait_recv()
             total = total + ss_last[q, peer]
-        return lax.rsqrt(total[:, :1] / (C * width) + norm_epsilon)
-
-    def finish(q, i, inverse):
+        scale[q] = lax.rsqrt(total / (C * width) + norm_epsilon)
+
+    def finish(q, i):
+        inverse = scale[q][:, :1]
         sums = []
         for which in range(2):
             value = second[q, i, which, y].astype(f32)
@@ -1066,13 +1068,9 @@
         return carry
 
     lax.fori_loop(0, steps, loop, 0)
-    project(0)
-    for n in range(kv, steps):
-        combine(n)
-
     pairs = [(i, which) for i in range(tiles) for which in range(2)]
 
-    def expand(q):
+    def expand(q, extra=None):
         gather(q)
         for n, (i, which) in enumerate(pairs):
             matmul(q, i, which)
@@ -1080,29 +1078,45 @@
                 middle_squares(q)
             if n:
                 middle(q, *pairs[n - 1])
+            if extra is not None and which:
+                extra(i)
         middle(q, *pairs[-1])
 
+    def finish_if(here, q, i):
+        @pl.when(here)
+        def _():
+            if i == 0:
+                inverse_rms(q)
+            finish(q, i)
+
     def contract(q):
-        inverse = inverse_rms(q)
+        forward(q, 0)
         for i in range(tiles):
-            finish(q, i, inverse)
-            if i:
-                forward(q, i - 1)
-        forward(q, tiles - 1)
-
-    near = jnp.logical_and(z - h <= 1, h - z <= 1)
-    always = z >= 0
-    spread(0, near)
-    project(1)
-    spread(0, jnp.logical_not(near))
-    expand(0)
-    spread(1, always)
-    expand(1)
-    for q in range(NQ):
-        contract(q)
-        for i in range(tiles):
+            if i + 1 < tiles:
+                forward(q, i + 1)
             down(q, i)
         scatter(q)
+
+    always = z >= 0
+    far = jnp.maximum(z - h, h - z)
+    early = z // CORES == y
+    late = z // CORES != y
+    project(0)
+    for n in range(kv, steps):
+        combine(n)
+    spread(0, far < 2)
+    spread(0, far == 2)
+    project(1)
+    spread(0, far > 2)
+    expand(0)
+    for i in range(tiles):
+        finish_if(late, 0, i)
+    spread(1, always)
+    expand(1, functools.partial(finish_if, early, 0))
+    contract(0)
+    for i in range(tiles):
+        finish_if(always, 1, i)
+    contract(1)
     for q in range(NQ):
         collect(q)
 
@@ -1143,7 +1157,7 @@
     NQ = row_count // 128
     RC = row_count // C // NQ
     rows = C * RC
-    NP = 2
+    NP = 4
     X = C // H
     Y = H // CORES
     hr = rows // H
@@ -1194,6 +1208,7 @@
             V((NQ, Y, hr, 128), f32),
             V((NQ, Y, hr, 128), f32),
             V((NQ, Y, hr, 128), f32),
+            V((NQ, hr, 128), f32),
             V((NQ, tiles, 2, CORES, Y, hr, tile), bf16),
             V((NQ, tiles, 2, Y, hr, tile), bf16),
             V((NQ, tiles, 2, Y, hr, tile), bf16),

time: 98.8 us -> 91 us (0.921)
  the two profiles are of different devices: /device:TPU:0 before, /device:TPU:9 now
where the time goes in v4:
time: 91 us; the launch traced here: 90 us
  Pallas kernels  88.4 us (97%)
  local copies, waits for them, and re-layouts  1.54 us (2%)
    pallas_call x1, Pallas kernels, fused(): pl.pallas_call(functools.partial(fused_kernel, C, H, NP), out_shape=jax.S...  88.4 us

profile of v4, /device:TPU:9, one launch (start us, length us, event | category | flops | bytes accessed | tf_op | source)
XLA Modules:
  0.0 90.0 jit_solution(18148082715487498319)
XLA Ops:
  0.0 88.4 %shard_map.109 = bf16[2,16,1344]{2,1,0:T(8,128)(2,1)} custom-call(s32[16]{0:T(128)} %map_hbm.1, s32[2,8]{1,0:T(2,128)} %sel_hbm.1, bf16[8,2,16,1024]{3,2,1,0:T(8,128)(2,1)} %bitcast.7, bf16[2,2,16,672]{3,2,1,0:T(8,128)(2,1)} %bitcast.9, f32[672]{0:T(1024)} %gain_hbm.1, bf16[2,2048,512]{2,1,0:T(8,128)(2,1)} %k_hbm.1, bf16[2,2048,512]{2,1,0:T(8,128)(2,1)} %v_hbm.1, ...), custom_call_target="tpu_custom_call" | custom-call | tf_op jit(solution)/shard_map/pallas_call | solution.py:1180
  88.4 1.5 %copy.13 = bf16[32,1344]{1,0:T(8,128)(2,1)} copy(bf16[32,1344]{1,0:T(8,128)(2,1)} %bitcast.8) | data formatting | bytes 172032

commit v5 on v4

--- a/solution.py
+++ b/solution.py
@@ -586,6 +586,7 @@
     ss_mid,
     ss_last,
     scale,
+    begun,
     first,
     first_in,
     second,
@@ -714,7 +715,7 @@
             ((ow_hbm, ow), (gw_hbm, gw), (uw_hbm, uw), (dw_hbm, dw))
         )
     ]
-    for load in inputs:
+    for load in inputs[:3]:
         load.wait()
 
     facts = []
@@ -903,9 +904,6 @@
             for i in range(NP):
                 block = u.at[q, source, pl.ds(i * RP, RP)]
                 arrived(block, u_r.at[q, source, i])
-        if q == 0:
-            loads[1].wait()
-            loads[2].wait()
         squares = 0.0
         for k in range(X):
             split = u[q, k, :, width:].astype(f32)
@@ -914,17 +912,27 @@
         ss_out[q] = squares.swapaxes(0, 1)
         send(ss_out.at[q, CORES - 1 - core], ss_in.at[q], ss_s.at[q, 0], ss_r.at[q, 0], c, partner)
 
+    def block_dot(q, k, i, which):
+        weight = (gw, uw)[which]
+        span = pl.ds(pl.multiple_of(k * width, 16), width)
+        return jnp.dot(
+            u[q, k, :, :width],
+            weight[span, i * tile : (i + 1) * tile],
+            preferred_element_type=f32,
+        )
+
+    def start_expand(q):
+        if q == 0:
+            loads[1].wait()
+            loads[2].wait()
+        for i in range(tiles):
+            for which in range(2):
+                begun[i, which] = block_dot(q, x, i, which)
+
     def matmul(q, i, which):
-        weight = (gw, uw)[which]
-        cols = slice(i * tile, (i + 1) * tile)
-        value = None
-        for k in range(X):
-            term = jnp.dot(
-                u[q, k, :, :width],
-                weight[k * width : (k + 1) * width, cols],
-                preferred_element_type=f32,
-            )
-            value = term if value is None else value + term
+        value = begun[i, which]
+        for d in range(1, X):
+            value = value + block_dot(q, (x + d) % X, i, which)
         value = value.reshape(Y, CORES, hr, tile).swapaxes(0, 1).astype(bf16)
         first[q, i, which] = value
         start(
@@ -1046,9 +1054,6 @@
         out_ref[q] = sum(part_in[q, k].astype(f32) for k in range(C)).astype(bf16)
 
     pl.semaphore_wait(barrier, C + H - 2)
-    send_if(visitor, res_ref, res_in.at[h], res_s.at[0], res_r.at[0], c, z)
-    res_in[h] = res_ref[...]
-
     steps = NQ * kv
     lag = 3
 
@@ -1068,9 +1073,14 @@
         return carry
 
     lax.fori_loop(0, steps, loop, 0)
+    for load in inputs[3:]:
+        load.wait()
+    send_if(visitor, res_ref, res_in.at[h], res_s.at[0], res_r.at[0], c, z)
+    res_in[h] = res_ref[...]
     pairs = [(i, which) for i in range(tiles) for which in range(2)]
 
     def expand(q, extra=None):
+        start_expand(q)
         gather(q)
         for n, (i, which) in enumerate(pairs):
             matmul(q, i, which)
@@ -1089,31 +1099,44 @@
                 inverse_rms(q)
             finish(q, i)
 
-    def contract(q):
-        forward(q, 0)
-        for i in range(tiles):
+    def contract(q, done=0):
+        forward(q, done)
+        for i in range(done, tiles):
             if i + 1 < tiles:
                 forward(q, i + 1)
             down(q, i)
         scatter(q)
+
+    def between(i):
+        finish_if(early, 0, i)
+        if i:
+
+            @pl.when(late)
+            def _():
+                forward(0, i - 1)
+                down(0, i - 1)
+
 
     always = z >= 0
     far = jnp.maximum(z - h, h - z)
     early = z // CORES == y
     late = z // CORES != y
     project(0)
-    for n in range(kv, steps):
+    for n in range(kv, steps - 2):
         combine(n)
-    spread(0, far < 2)
-    spread(0, far == 2)
+    spread(0, far == 0)
+    for n in range(steps - 2, steps):
+        combine(n)
+    spread(0, far == 1)
     project(1)
-    spread(0, far > 2)
+    spread(0, far > 1)
     expand(0)
     for i in range(tiles):
         finish_if(late, 0, i)
     spread(1, always)
-    expand(1, functools.partial(finish_if, early, 0))
-    contract(0)
+    expand(1, between)
+    pl.when(late)(lambda: contract(0, tiles - 1))
+    pl.when(early)(lambda: contract(0))
     for i in range(tiles):
         finish_if(always, 1, i)
     contract(1)
@@ -1209,6 +1232,7 @@
             V((NQ, Y, hr, 128), f32),
             V((NQ, Y, hr, 128), f32),
             V((NQ, hr, 128), f32),
+            V((tiles, 2, rows, tile), f32),
             V((NQ, tiles, 2, CORES, Y, hr, tile), bf16),
             V((NQ, tiles, 2, Y, hr, tile), bf16),
             V((NQ, tiles, 2, Y, hr, tile), bf16),

time: 91 us -> 88 us (0.967)
  Pallas kernels: 88.4 us -> 84.7 us
    pallas_call x1, Pallas kernels: 88.4 us -> 84.7 us  [fused(): pl.pallas_call(functools.partial(fused_kernel, C, H, NP), out_shape=jax.S...]
where the time goes in v5:
time: 88 us; the launch traced here: 86.2 us
  Pallas kernels  84.7 us (96%)
  local copies, waits for them, and re-layouts  1.54 us (2%)
    pallas_call x1, Pallas kernels, fused(): pl.pallas_call(functools.partial(fused_kernel, C, H, NP), out_shape=jax.S...  84.7 us

profile of v5, /device:TPU:9, one launch (start us, length us, event | category | flops | bytes accessed | tf_op | source)
XLA Modules:
  0.0 86.2 jit_solution(45762178917212206)
XLA Ops:
  0.0 84.7 %shard_map.109 = bf16[2,16,1344]{2,1,0:T(8,128)(2,1)} custom-call(s32[16]{0:T(128)} %map_hbm.1, s32[2,8]{1,0:T(2,128)} %sel_hbm.1, bf16[8,2,16,1024]{3,2,1,0:T(8,128)(2,1)} %bitcast.7, bf16[2,2,16,672]{3,2,1,0:T(8,128)(2,1)} %bitcast.9, f32[672]{0:T(1024)} %gain_hbm.1, bf16[2,2048,512]{2,1,0:T(8,128)(2,1)} %k_hbm.1, bf16[2,2048,512]{2,1,0:T(8,128)(2,1)} %v_hbm.1, ...), custom_call_target="tpu_custom_call" | custom-call | tf_op jit(solution)/shard_map/pallas_call | solution.py:1203
  84.7 1.5 %copy.13 = bf16[32,1344]{1,0:T(8,128)(2,1)} copy(bf16[32,1344]{1,0:T(8,128)(2,1)} %bitcast.8) | data formatting | bytes 172032

commit v6 on v5

--- a/solution.py
+++ b/solution.py
@@ -604,6 +604,7 @@
     lse_r,
     att_s,
     att_r,
+    cross_r,
     po_s,
     po_r,
     res_s,
@@ -706,9 +707,8 @@
     ]
     for load in inputs:
         load.start()
-    for j in range(kv):
-        for load in kv_load(j):
-            load.start()
+    for load in kv_load(0):
+        load.start()
     loads = [
         pltpu.make_async_copy(src, dst, w_sem.at[i])
         for i, (src, dst) in enumerate(
@@ -752,6 +752,9 @@
 
         @pl.when(n == 0)
         def _():
+            for k in range(1, kv):
+                for load in kv_load(k):
+                    load.start()
             for load in loads:
                 load.start()
 
@@ -803,10 +806,23 @@
             remote(mix_out.at[n, peer], mix_in.at[n, c], mix_s.at[0], mix_r.at[n], peer, h).start()
             remote(lse_out.at[n], lse_in.at[n, c], lse_s.at[0], lse_r.at[n], peer, h).start()
 
-    def att_sends(n):
-        for d in range(1, C):
-            peer = (c + d) % C
-            remote(att.at[n, c], att.at[n, c], att_s.at[0], att_r.at[n], peer, h).start()
+    def att_sends(n, direct):
+        block = att.at[n, c]
+        if direct:
+            for d in range(1, C):
+                start(block, block, att_s.at[0], att_r.at[n], (c + d) % C, h)
+        else:
+            for d in range(1, Z):
+                start(block, block, att_s.at[0], att_r.at[n], (z + d) % Z * X + x, h)
+            for d in range(1, X):
+                start(block, block, att_s.at[0], cross_r.at[n - kv], z * X + (x + d) % X, h)
+
+    def att_relay(n):
+        arrived(att.at[n, pl.ds(0, Z - 1)], att_r.at[n])
+        for e in range(1, Z):
+            block = att.at[n, (z + e) % Z * X + x]
+            for d in range(1, X):
+                start(block, block, att_s.at[0], cross_r.at[n - kv], z * X + (x + d) % X, h)
 
     def arrived(block, recv_sem):
         remote(block, block, recv_sem, recv_sem, c, partner).wait_recv()
@@ -814,7 +830,7 @@
     def left(block, send_sem):
         remote(block, block, send_sem, send_sem, c, partner).wait_send()
 
-    def combine(n):
+    def combine(n, direct):
         arrived(lse_in.at[n, pl.ds(0, C - 1)], lse_r.at[n])
         arrived(mix_in.at[n, pl.ds(0, C - 1)], mix_r.at[n])
         logs = [lse_in[n, k] for k in range(C)]
@@ -831,12 +847,15 @@
                 share = jnp.sum(jnp.where(mine, share, 0.0), axis=1, keepdims=True)
                 value = value + share * mix_in[n, k, :, cols].astype(f32)
             att[n, c, :, cols] = value.astype(bf16)
-        att_sends(n)
+        att_sends(n, direct)
 
     def project(q):
         for j in range(kv):
             n = q * kv + j
-            arrived(att.at[n, pl.ds(0, C - 1)], att_r.at[n])
+            if q == 0:
+                arrived(att.at[n, pl.ds(0, C - 1)], att_r.at[n])
+            else:
+                arrived(att.at[n, pl.ds(0, (X - 1) * Z)], cross_r.at[n - kv])
         if q == 0:
             loads[0].wait()
         value = None
@@ -883,15 +902,18 @@
         piece = u.at[q, x, pl.ds(i * RP, RP)]
         recv = u_r.at[q, x, i]
         pl.when(jnp.logical_and(here, visitor))(functools.partial(arrived, piece, recv))
-        up = jnp.logical_and(here, jnp.logical_and(z >= h, z < Z - 1))
-        down = jnp.logical_and(here, jnp.logical_and(z <= h, z > 0))
-        above = jnp.minimum(z + 1, Z - 1) * X + x
-        below = jnp.maximum(z - 1, 0) * X + x
-        send_if(up, piece, piece, u_s.at[q, i, 0], recv, above, h)
-        send_if(down, piece, piece, u_s.at[q, i, 1], recv, below, h)
+        for way, ahead in enumerate((Z - 1 - z, z)):
+            step = 1 - 2 * way
+            go = jnp.logical_and(jnp.logical_and(here, step * (z - h) >= 0), ahead > 0)
+            target = jnp.clip(z + step, 0, Z - 1) * X + x
+            copy = remote(piece, piece, u_s.at[way], recv, target, h)
+            pl.when(go)(copy.start)
+            kept.append((go, copy))
         for d in range(1, X):
             peer = z * X + (x + d) % X
-            send_if(here, piece, piece, u_s.at[q, i, 1 + d], recv, peer, h)
+            copy = remote(piece, piece, u_s.at[1 + d], recv, peer, h)
+            pl.when(here)(copy.start)
+            kept.append((here, copy))
 
     def spread(q, here):
         for i in range(NP):
@@ -1053,17 +1075,25 @@
         arrived(part_in.at[q, pl.ds(0, C - 1)], part_r.at[q])
         out_ref[q] = sum(part_in[q, k].astype(f32) for k in range(C)).astype(bf16)
 
-    pl.semaphore_wait(barrier, C + H - 2)
     steps = NQ * kv
     lag = 3
 
     def loop(n, carry):
         attend(n)
-        pl.when(jnp.logical_or(n < kv, n >= kv + lag))(functools.partial(mix_sends, n))
-
-        @pl.when(jnp.logical_and(n >= lag, n < kv + lag))
+
+        @pl.when(n == 1)
         def _():
-            combine(n - lag)
+            pl.semaphore_wait(barrier, C + H - 2)
+            mix_sends(0)
+
+        ready = jnp.logical_and(n >= 1, n < kv)
+        pl.when(jnp.logical_or(ready, n >= kv + lag))(functools.partial(mix_sends, n))
+
+        for k in range(kv):
+
+            @pl.when(n == (kv + lag - 2 if k == kv - 1 else max(k + 2, lag)))
+            def _(k=k):
+                combine(k, True)
 
         @pl.when(n == kv + lag - 1)
         def _():
@@ -1117,28 +1147,37 @@
                 down(0, i - 1)
 
 
-    always = z >= 0
     far = jnp.maximum(z - h, h - z)
     early = z // CORES == y
     late = z // CORES != y
     project(0)
     for n in range(kv, steps - 2):
-        combine(n)
+        combine(n, False)
     spread(0, far == 0)
     for n in range(steps - 2, steps):
-        combine(n)
+        combine(n, False)
+    for n in range(kv, steps - 2):
+        att_relay(n)
     spread(0, far == 1)
+    for n in range(steps - 2, steps):
+        att_relay(n)
+    spread(0, far == 2)
     project(1)
-    spread(0, far > 1)
-    expand(0)
+    spread(0, far > 2)
+    expand(0, lambda i: spread(1, far == 0) if i == tiles - 2 else None)
+    first_on = jnp.logical_and(late, far <= 2)
+    spread(1, first_on)
     for i in range(tiles):
         finish_if(late, 0, i)
-    spread(1, always)
+    spread(1, jnp.logical_and(jnp.logical_not(first_on), far > 0))
     expand(1, between)
+    for i in range(tiles - 1):
+        finish_if(late, 1, i)
     pl.when(late)(lambda: contract(0, tiles - 1))
+    finish_if(late, 1, tiles - 1)
     pl.when(early)(lambda: contract(0))
     for i in range(tiles):
-        finish_if(always, 1, i)
+        finish_if(early, 1, i)
     contract(1)
     for q in range(NQ):
         collect(q)
@@ -1250,11 +1289,12 @@
             S((steps,)),
             S((1,)),
             S((steps,)),
+            S((kv,)),
             S((NQ,)),
             S((NQ, NP)),
             S((1,)),
             S((1,)),
-            S((NQ, NP, 1 + X)),
+            S((1 + X,)),
             S((NQ, X, NP)),
             S((NQ, Y)),
             S((NQ, 1 + Y)),

time: 88 us -> 85.5 us (0.972); the launches traced: 86.2 us -> 85.2 us
  Pallas kernels: 84.7 us -> 83.7 us
    pallas_call x1, Pallas kernels: 84.7 us -> 83.7 us  [fused(): pl.pallas_call(functools.partial(fused_kernel, C, H, NP), out_shape=jax.S...]
where the time goes in v6:
time: 85.5 us; the launch traced here: 85.2 us
  Pallas kernels  83.7 us (98%)
  local copies, waits for them, and re-layouts  1.54 us (2%)
    pallas_call x1, Pallas kernels, fused(): pl.pallas_call(functools.partial(fused_kernel, C, H, NP), out_shape=jax.S...  83.7 us

profile of v6, /device:TPU:9, one launch (start us, length us, event | category | flops | bytes accessed | tf_op | source)
XLA Modules:
  0.0 85.2 jit_solution(16133123281388163720)
XLA Ops:
  0.0 83.7 %shard_map.109 = bf16[2,16,1344]{2,1,0:T(8,128)(2,1)} custom-call(s32[16]{0:T(128)} %map_hbm.1, s32[2,8]{1,0:T(2,128)} %sel_hbm.1, bf16[8,2,16,1024]{3,2,1,0:T(8,128)(2,1)} %bitcast.7, bf16[2,2,16,672]{3,2,1,0:T(8,128)(2,1)} %bitcast.9, f32[672]{0:T(1024)} %gain_hbm.1, bf16[2,2048,512]{2,1,0:T(8,128)(2,1)} %k_hbm.1, bf16[2,2048,512]{2,1,0:T(8,128)(2,1)} %v_hbm.1, ...), custom_call_target="tpu_custom_call" | custom-call | tf_op jit(solution)/shard_map/pallas_call | solution.py:1242
  83.7 1.5 %copy.13 = bf16[32,1344]{1,0:T(8,128)(2,1)} copy(bf16[32,1344]{1,0:T(8,128)(2,1)} %bitcast.8) | data formatting | bytes 172032

commit v7 on v6

--- a/solution.py
+++ b/solution.py
@@ -1110,7 +1110,6 @@
     pairs = [(i, which) for i in range(tiles) for which in range(2)]
 
     def expand(q, extra=None):
-        start_expand(q)
         gather(q)
         for n, (i, which) in enumerate(pairs):
             matmul(q, i, which)
@@ -1161,15 +1160,18 @@
     spread(0, far == 1)
     for n in range(steps - 2, steps):
         att_relay(n)
+    pl.when(far <= 1)(lambda: start_expand(0))
     spread(0, far == 2)
     project(1)
     spread(0, far > 2)
-    expand(0, lambda i: spread(1, far == 0) if i == tiles - 2 else None)
+    pl.when(far > 1)(lambda: start_expand(0))
+    expand(0, lambda i: spread(1, far == 0) if i == tiles - 1 else None)
     first_on = jnp.logical_and(late, far <= 2)
     spread(1, first_on)
     for i in range(tiles):
         finish_if(late, 0, i)
     spread(1, jnp.logical_and(jnp.logical_not(first_on), far > 0))
+    start_expand(1)
     expand(1, between)
     for i in range(tiles - 1):
         finish_if(late, 1, i)
@@ -1241,7 +1243,7 @@
     mixes = V((steps, C, RC, group * HEAD_SIZE), bf16)
     return pl.pallas_call(
         functools.partial(fused_kernel, C, H, NP),
-        out_shape=jax.ShapeDtypeStruct((NQ, RC, out_width), bf16),
+        out_shape=pltpu.VMEM((NQ, RC, out_width), bf16),
         in_specs=[hbm] * 11,
         out_specs=vmem,
         scratch_shapes=[

time: 85.5 us -> 83.7 us (0.979)
  local copies, waits for them, and re-layouts: 1.54 us -> 0.64 us
    unnamed x1, local copies, waits for them, and re-layouts: 1.54 us -> 0.64 us
where the time goes in v7:
time: 83.7 us; the launch traced here: 83.6 us
  Pallas kernels  82.9 us (99%)
    pallas_call x1, Pallas kernels, fused(): pl.pallas_call(functools.partial(fused_kernel, C, H, NP), out_shape=pltpu...  82.9 us

profile of v7, /device:TPU:9, one launch (start us, length us, event | category | flops | bytes accessed | tf_op | source)
XLA Modules:
  0.0 83.6 jit_solution(16316564907302876529)
XLA Ops:
  0.0 82.9 %shard_map.109 = bf16[2,16,1344]{2,1,0:T(8,128)(2,1)S(1)} custom-call(s32[16]{0:T(128)} %map_hbm.1, s32[2,8]{1,0:T(2,128)} %sel_hbm.1, bf16[8,2,16,1024]{3,2,1,0:T(8,128)(2,1)} %bitcast.8, bf16[2,2,16,672]{3,2,1,0:T(8,128)(2,1)} %bitcast.9, f32[672]{0:T(1024)} %gain_hbm.1, bf16[2,2048,512]{2,1,0:T(8,128)(2,1)} %k_hbm.1, bf16[2,2048,512]{2,1,0:T(8,128)(2,1)} %v_hbm.1, ...), custom_call_target="tpu_custom_call" | custom-call | tf_op jit(solution)/shard_map/pallas_call | solution.py:1244
  82.9 0.6 copy.13

commit v8 on v7

--- a/solution.py
+++ b/solution.py
@@ -881,10 +881,10 @@
             arrived(res_in.at[pl.ds(0, H - 1)], res_r.at[0])
         arrived(po_in.at[q, pl.ds(0, H - 1), pl.ds(i * RP, RP)], po_r.at[q, i])
         spare = u.shape[-1] - width
-        lane = lax.broadcasted_iota(jnp.int32, (hr, spare), 1)
-        for b in range(i * RP // hr, (i + 1) * RP // hr):
-            span = slice(b * hr, (b + 1) * hr)
-            value = res_in[b, :, q].reshape(hr, width).astype(f32)
+        lane = lax.broadcasted_iota(jnp.int32, (RC, spare), 1)
+        for b in range(i * RP // RC, (i + 1) * RP // RC):
+            span = slice(b * RC, (b + 1) * RC)
+            value = res_in[b // X, b % X, q].astype(f32)
             added = sum(po_in[q, k, span].astype(f32) for k in range(H))
             stream = (value + added).astype(bf16)
             st[q, span] = stream
@@ -1087,7 +1087,7 @@
             mix_sends(0)
 
         ready = jnp.logical_and(n >= 1, n < kv)
-        pl.when(jnp.logical_or(ready, n >= kv + lag))(functools.partial(mix_sends, n))
+        pl.when(jnp.logical_or(ready, n >= kv + lag - 1))(functools.partial(mix_sends, n))
 
         for k in range(kv):
 
@@ -1095,9 +1095,9 @@
             def _(k=k):
                 combine(k, True)
 
-        @pl.when(n == kv + lag - 1)
+        @pl.when(n == kv + lag - 2)
         def _():
-            for k in range(kv, kv + lag):
+            for k in range(kv, kv + lag - 1):
                 mix_sends(k)
 
         return carry
@@ -1221,7 +1221,7 @@
     NQ = row_count // 128
     RC = row_count // C // NQ
     rows = C * RC
-    NP = 4
+    NP = 8
     X = C // H
     Y = H // CORES
     hr = rows // H

time: 83.7 us -> 83.4 us (level)
  no operation moved by 1% of the time
where the time goes in v8:
time: 83.4 us; the launch traced here: 83.3 us
  Pallas kernels  82.6 us (99%)
    pallas_call x1, Pallas kernels, fused(): pl.pallas_call(functools.partial(fused_kernel, C, H, NP), out_shape=pltpu...  82.6 us

profile of v8, /device:TPU:9, one launch (start us, length us, event | category | flops | bytes accessed | tf_op | source)
XLA Modules:
  0.0 83.3 jit_solution(12200041600256606071)
XLA Ops:
  0.0 82.6 %shard_map.109 = bf16[2,16,1344]{2,1,0:T(8,128)(2,1)S(1)} custom-call(s32[16]{0:T(128)} %map_hbm.1, s32[2,8]{1,0:T(2,128)} %sel_hbm.1, bf16[8,2,16,1024]{3,2,1,0:T(8,128)(2,1)} %bitcast.8, bf16[2,2,16,672]{3,2,1,0:T(8,128)(2,1)} %bitcast.9, f32[672]{0:T(1024)} %gain_hbm.1, bf16[2,2048,512]{2,1,0:T(8,128)(2,1)} %k_hbm.1, bf16[2,2048,512]{2,1,0:T(8,128)(2,1)} %v_hbm.1, ...), custom_call_target="tpu_custom_call" | custom-call | tf_op jit(solution)/shard_map/pallas_call | solution.py:1244
  82.6 0.6 copy.13

commit v9 on v7

--- a/solution.py
+++ b/solution.py
@@ -1087,7 +1087,7 @@
             mix_sends(0)
 
         ready = jnp.logical_and(n >= 1, n < kv)
-        pl.when(jnp.logical_or(ready, n >= kv + lag))(functools.partial(mix_sends, n))
+        pl.when(jnp.logical_or(ready, n >= kv + lag - 1))(functools.partial(mix_sends, n))
 
         for k in range(kv):
 
@@ -1095,9 +1095,9 @@
             def _(k=k):
                 combine(k, True)
 
-        @pl.when(n == kv + lag - 1)
+        @pl.when(n == kv + lag - 2)
         def _():
-            for k in range(kv, kv + lag):
+            for k in range(kv, kv + lag - 1):
                 mix_sends(k)
 
         return carry

time: 83.7 us -> 83.6 us (level)
  no operation moved by 1% of the time
where the time goes in v9:
time: 83.6 us; the launch traced here: 83.4 us
  Pallas kernels  82.8 us (99%)
    pallas_call x1, Pallas kernels, fused(): pl.pallas_call(functools.partial(fused_kernel, C, H, NP), out_shape=pltpu...  82.8 us

profile of v9, /device:TPU:9, one launch (start us, length us, event | category | flops | bytes accessed | tf_op | source)
XLA Modules:
  0.0 83.4 jit_solution(4339973415934793394)
XLA Ops:
  0.0 82.8 %shard_map.109 = bf16[2,16,1344]{2,1,0:T(8,128)(2,1)S(1)} custom-call(s32[16]{0:T(128)} %map_hbm.1, s32[2,8]{1,0:T(2,128)} %sel_hbm.1, bf16[8,2,16,1024]{3,2,1,0:T(8,128)(2,1)} %bitcast.8, bf16[2,2,16,672]{3,2,1,0:T(8,128)(2,1)} %bitcast.9, f32[672]{0:T(1024)} %gain_hbm.1, bf16[2,2048,512]{2,1,0:T(8,128)(2,1)} %k_hbm.1, bf16[2,2048,512]{2,1,0:T(8,128)(2,1)} %v_hbm.1, ...), custom_call_target="tpu_custom_call" | custom-call | tf_op jit(solution)/shard_map/pallas_call | solution.py:1244
  82.8 0.6 copy.13
